TPU v7x, 256 devices: a whole 4x4x8 slice. The times are simulated.
256 devices in a mesh: dp: 32 (over x, y, core), table: 8 (over z).
Axes of the slice: x: 4, y: 4, z: 8, core: 2. Of those that a mesh axis runs over, the one named last changes fastest.
Arguments:
- item_ids: int32 [512, 384], P(('dp', 'table')), may hold values from 0 to 3145727, as said below
- table_ids: int32 [512, 384], P(('dp', 'table')), may hold values from 0 to 3
- lengths: int32 [512], P(('dp', 'table')), may hold values from 24 to 384
- assignment: int32 [512], P(('dp', 'table')), may hold values from 0 to 511, as said below
- table_a: bfloat16 [3145728, 64], P(('dp', 'table')), may hold values from -6 to 6
- table_b: bfloat16 [3145728, 64], P(('dp', 'table')), may hold values from -6 to 6
- table_c: bfloat16 [1572864, 128], P(('dp', 'table')), may hold values from -6 to 6
- table_d: bfloat16 [524288, 256], P(('dp', 'table')), may hold values from -6 to 6
- proj_weight: bfloat16 [512, 512], P('dp'), may hold values from -0.5 to 0.5
- in_weight: bfloat16 [512, 2048], P('dp'), may hold values from -0.25 to 0.25
- out_weight: bfloat16 [512, 512], P('dp'), may hold values from -0.25 to 0.25
- cotangent: bfloat16 [512, 384, 512], P(('dp', 'table')), may hold values from -24 to 24
Outputs:
- output: bfloat16 [512, 384, 512], P(('dp', 'table'))
- grad_a: bfloat16 [3145728, 64], P(('dp', 'table'))
- grad_b: bfloat16 [3145728, 64], P(('dp', 'table'))
- grad_c: bfloat16 [1572864, 128], P(('dp', 'table'))
- grad_d: bfloat16 [524288, 256], P(('dp', 'table'))
- grad_proj: float32 [512, 512], P('dp')
- grad_in: float32 [512, 2048], P('dp')
- grad_out: float32 [512, 512], P('dp')
Inputs may be any that keep to these rules, and one draw needn't show every extreme that they name: `item_ids`: A sequence's events past its length name rows too. An event's item is below 256 times the rows one device holds of the event's table (row r of a table lies on device r // (rows a device of that table) along dp+table). After the move, the events of the 2 slots of one device name at most 2 times rows of one table held by one device, and for some table and device exactly 2 times, from every device. `assignment`: A permutation of the sequence slots; a sequence moves only among the devices of its own table index, and each device receives 2 sequences.
All inputs are finite; a program needn't handle non-finite values.
Results may differ from a plain program's by a relative error of at most 0.028.
Values may be sent and summed in bfloat16 or wider, within the bound.
A program may use at most 128 MiB of HBM per device.

v0:
```python
import functools

import jax
import jax.numpy as jnp
from jax import lax
from jax.experimental import pallas as pl
from jax.experimental.pallas import tpu as pltpu
from jax.sharding import PartitionSpec as P

MESH = pl.DeviceIdType.MESH
VM = pl.BlockSpec(memory_space=pltpu.VMEM)
F32, BF16, I32 = jnp.float32, jnp.bfloat16, jnp.int32
NX, NY, NZ, PLANE = 4, 4, 8, 16
DEVICES = 256
HEADS, HEAD = 4, 128
SPAN, TOKENS, WIDTH = 384, 768, 512
ROWS = (12288, 12288, 6144, 2048)
FOLD = (4, 4, 2, 1)
TABLE_BITS = 22
KEY = 1024
NONE = 16383.0 * KEY
VMEM_LIMIT = 60 << 20


def place():
    dp, z = lax.axis_index("dp"), lax.axis_index("table")
    return dp, dp // 2, lax.rem(dp, 2), z


def plane_peer(xy, k):
    x = lax.rem(xy // NY + k // NY, NX)
    y = lax.rem(lax.rem(xy, NY) + k % NY, NY)
    return x * NY + y


def peers():
    dp, xy, core, z = place()
    along_z = [(dp, lax.rem(z + k, NZ)) for k in range(1, NZ)]
    in_plane = [(plane_peer(xy, k) * 2 + core, z) for k in range(1, PLANE)]
    return along_z, in_plane, [(xy * 2 + (1 - core), z)]


def near():
    dp, xy, core, z = place()
    x, y = xy // NY, lax.rem(xy, NY)
    right, left = lax.rem(x + 1, NX), lax.rem(x + NX - 1, NX)
    up, down = lax.rem(y + 1, NY), lax.rem(y + NY - 1, NY)

    def at(px, py):
        return ((px * NY + py) * 2 + core, z)

    return (x, right, left, at(right, y), at(left, y)), (y, up, down, at(x, up), at(x, down))


def greet(targets):
    barrier = pltpu.get_barrier_semaphore()
    for dp, z in targets:
        pl.semaphore_signal(barrier, inc=1, device_id=(dp, z), device_id_type=MESH)
    pl.semaphore_wait(barrier, len(targets))


def send(src, dst, send_sem, recv_sem, target):
    copy = pltpu.make_async_remote_copy(
        src_ref=src,
        dst_ref=dst,
        send_sem=send_sem,
        recv_sem=recv_sem,
        device_id=target,
        device_id_type=MESH,
    )
    copy.start()
    return copy


def dot(a, b, da=1, db=0):
    return lax.dot_general(a, b, (((da,), (db,)), ((), ())), preferred_element_type=F32)


def share_kernel(x_ref, w_ref, ids_ref, full_ref, send_sem, recv_sem, own_sem):
    dp, xy, core, z = place()
    (x, right, left, to_right, to_left), (y, up, down, to_up, to_down) = near()
    own = [
        pltpu.make_async_copy(x_ref, ids_ref.at[x, y, core, z], own_sem.at[0]),
        pltpu.make_async_copy(w_ref, full_ref.at[x, y, core], own_sem.at[1]),
    ]
    for copy in own:
        copy.start()
    along_z, _plane, partner = peers()
    greet(along_z + [to_right, to_left, to_up, to_down] + partner)
    used = [0]

    def start(src, dst, target):
        at = used[0]
        used[0] += 1
        return send(src, dst, send_sem.at[at], recv_sem.at[at], target)

    def move(ref, target):
        return start(ref, ref, target)

    def finish(copies):
        for copy in copies:
            copy.wait()

    def w(px, py, part):
        return full_ref.at[px, py, core, part]

    def ids(px, py, low, count):
        return ids_ref.at[px, py, core, pl.ds(low, count)]

    every, low, high = slice(None), pl.ds(0, 2), pl.ds(2, 2)
    first = [start(x_ref, ids_ref.at[x, y, core, z], t) for t in along_z]
    w_one = [
        start(w_ref.at[0], w(x, y, 0), to_up),
        start(w_ref.at[0], w(x, y, 0), to_down),
        start(w_ref.at[1], w(x, y, 1), to_right),
        start(w_ref.at[1], w(x, y, 1), to_left),
    ]
    finish(own + w_one)
    ahead, behind = pl.ds(0, 1536), pl.ds(1536, 1536)
    w_two = [
        move(full_ref.at[x, down, core, 0, :, ahead], to_up),
        move(full_ref.at[x, up, core, 0, :, behind], to_down),
        move(full_ref.at[left, y, core, 1, :, ahead], to_right),
        move(full_ref.at[right, y, core, 1, :, behind], to_left),
    ]
    finish(first)
    i_one = [
        move(ids(x, y, 0, 4), to_up),
        move(ids(x, y, 0, 4), to_down),
        move(ids(x, y, 4, 4), to_right),
        move(ids(x, y, 4, 4), to_left),
    ]
    finish(w_two)
    w_three = [
        move(w(x, every, 0), to_right),
        move(w(x, every, 0), to_left),
        move(w(every, y, 1), to_up),
        move(w(every, y, 1), to_down),
    ]
    finish(i_one)
    i_two = [
        move(ids(x, down, 0, 2), to_up),
        move(ids(x, up, 2, 2), to_down),
        move(ids(left, y, 4, 2), to_right),
        move(ids(right, y, 6, 2), to_left),
    ]
    finish(i_two)
    i_three = [
        move(ids(x, every, 0, 4), to_right),
        move(ids(x, every, 0, 4), to_left),
        move(ids(every, y, 4, 4), to_up),
        move(ids(every, y, 4, 4), to_down),
    ]
    finish(w_three)
    w_four = [
        move(w(left, low, 0), to_right),
        move(w(right, high, 0), to_left),
        move(w(low, down, 1), to_up),
        move(w(high, up, 1), to_down),
    ]
    finish(i_three)
    i_four = [
        move(ids(left, low, 0, 4), to_right),
        move(ids(right, high, 0, 4), to_left),
        move(ids(low, down, 4, 4), to_up),
        move(ids(high, up, 4, 4), to_down),
    ]
    finish(w_four)
    last = [move(full_ref.at[:, :, core], partner[0])]
    finish(i_four)
    last.append(move(ids_ref.at[:, :, core], partner[0]))
    finish(last)


def share(words, weights):
    columns = weights.shape[-1]
    return pl.pallas_call(
        share_kernel,
        out_shape=(
            jax.ShapeDtypeStruct((NX, NY, 2, NZ, 8, 128), I32),
            jax.ShapeDtypeStruct((NX, NY, 2, 2, 8, columns), BF16),
        ),
        in_specs=[VM, VM],
        out_specs=(VM, VM),
        scratch_shapes=[
            pltpu.SemaphoreType.DMA((41,)),
            pltpu.SemaphoreType.DMA((41,)),
            pltpu.SemaphoreType.DMA((2,)),
        ],
        compiler_params=pltpu.CompilerParams(
            collective_id=1, has_side_effects=True, vmem_limit_bytes=VMEM_LIMIT
        ),
        name="share",
    )(words, weights)


def swap_kernel(x_ref, out_ref, by_z, from_z, by_dp, from_dp, again_dp, again_z, final_z, send_sem, recv_sem):
    dp, xy, core, z = place()
    along_z, in_plane, partner = peers()
    others = [(plane_peer(xy, k) * 2 + (1 - core), z) for k in range(1, PLANE)]
    along_dp = in_plane + partner + others
    greet(along_z + along_dp)
    i = lax.broadcasted_iota(I32, (DEVICES, DEVICES), 0)
    j = lax.broadcasted_iota(I32, (DEVICES, DEVICES), 1)
    z_first = (j == (i & 31) * 8 + (i >> 5)).astype(BF16)
    dp_first = (j == (i & 7) * 32 + (i >> 3)).astype(BF16)

    def arrange(matrix, ref, dims):
        return dot(matrix, ref.reshape(DEVICES, 512)).astype(BF16).reshape(dims)

    by_dp[...] = x_ref[:, 512:1024].reshape(32, 8, 512)
    low = [
        send(by_dp.at[t[0]], from_dp.at[dp], send_sem.at[n], recv_sem.at[n], t)
        for n, t in enumerate(along_dp)
    ]
    by_z[...] = arrange(z_first, x_ref[:, 0:512], (8, 32, 512))
    high = [
        send(by_z.at[t[1]], from_z.at[z], send_sem.at[31 + n], recv_sem.at[31 + n], t)
        for n, t in enumerate(along_z)
    ]
    from_dp[pl.ds(dp, 1)] = by_dp[pl.ds(dp, 1)]
    from_z[pl.ds(z, 1)] = by_z[pl.ds(z, 1)]
    for copy in low:
        copy.wait()
    again_z[...] = arrange(z_first, from_dp[...], (8, 32, 512))
    low = [
        send(again_z.at[t[1]], final_z.at[z], send_sem.at[38 + n], recv_sem.at[38 + n], t)
        for n, t in enumerate(along_z)
    ]
    final_z[pl.ds(z, 1)] = again_z[pl.ds(z, 1)]
    for copy in high:
        copy.wait()
    again_dp[...] = arrange(dp_first, from_z[...], (32, 8, 512))
    high = [
        send(again_dp.at[t[0]], out_ref.at[0, dp], send_sem.at[45 + n], recv_sem.at[45 + n], t)
        for n, t in enumerate(along_dp)
    ]
    out_ref[0, pl.ds(dp, 1)] = again_dp[pl.ds(dp, 1)]
    for copy in low:
        copy.wait()
    out_ref[1] = arrange(dp_first, final_z[...], (32, 8, 512))
    for copy in high:
        copy.wait()


def swap(rows):
    return pl.pallas_call(
        swap_kernel,
        out_shape=jax.ShapeDtypeStruct((2, 32, 8, 512), BF16),
        in_specs=[VM],
        out_specs=VM,
        scratch_shapes=[
            pltpu.VMEM((8, 32, 512), BF16),
            pltpu.VMEM((8, 32, 512), BF16),
            pltpu.VMEM((32, 8, 512), BF16),
            pltpu.VMEM((32, 8, 512), BF16),
            pltpu.VMEM((32, 8, 512), BF16),
            pltpu.VMEM((8, 32, 512), BF16),
            pltpu.VMEM((8, 32, 512), BF16),
            pltpu.SemaphoreType.DMA((76,)),
            pltpu.SemaphoreType.DMA((76,)),
        ],
        compiler_params=pltpu.CompilerParams(
            collective_id=2, has_side_effects=True, vmem_limit_bytes=VMEM_LIMIT
        ),
        name="swap",
    )(rows)


def smallest_two(keys):
    first = jnp.full((8, keys.shape[1]), NONE, F32)
    second = first
    for at in range(0, keys.shape[0], 8):
        value = keys[at : at + 8]
        second = jnp.minimum(second, jnp.maximum(first, value))
        first = jnp.minimum(first, value)
    low = jnp.min(first, axis=0, keepdims=True)
    high = jnp.min(jnp.where(first == low, second, first), axis=0, keepdims=True)
    return low, high


def lookup_kernel(me_ref, ids_ref, a_ref, b_ref, c_ref, d_ref, send_ref, wanted_ref, cols_ref, moved):
    me = me_ref[0]
    words = jnp.concatenate(
        [
            jnp.concatenate([ids_ref[:, 4 * s + r, :] for r in range(3)], axis=1)
            for s in range(2)
        ],
        axis=0,
    )
    extra = jnp.concatenate([ids_ref[:, 3, :], ids_ref[:, 7, :]], axis=0)
    lengths = extra[:, 0:1].astype(F32)
    targets = extra[:, 1:2]
    arranged = (targets & 1) * DEVICES + (targets >> 1)
    slots = lax.broadcasted_iota(I32, (512, 512), 1)
    goes = (arranged == slots).astype(BF16)
    total = None
    for shift in (16, 8, 0):
        part = ((words >> shift) & 255).astype(F32).astype(BF16)
        piece = dot(part, goes, 0, 0)
        total = piece if total is None else total * 256.0 + piece
    moved[...] = total

    place_of = lax.broadcasted_iota(I32, (SPAN, 512), 0).astype(F32)
    lows, highs = [], []
    for which in range(4):
        start = which * (1 << TABLE_BITS) + me * ROWS[which]
        local = moved[...] - start.astype(F32)
        held = (local >= 0.0) & (local < float(ROWS[which]))
        keys = jnp.where(held, local * float(KEY) + place_of, NONE)
        low, high = smallest_two(keys)
        low_a, high_a = low[:, :DEVICES], high[:, :DEVICES]
        low_b, high_b = low[:, DEVICES:] + float(SPAN), high[:, DEVICES:] + float(SPAN)
        lows.append(jnp.minimum(low_a, low_b))
        highs.append(jnp.minimum(jnp.maximum(low_a, low_b), jnp.minimum(high_a, high_b)))
    row_form = jnp.floor(jnp.concatenate(lows + highs, axis=0) * (1.0 / KEY))
    wanted_ref[...] = row_form
    padded = jnp.concatenate([row_form, jnp.zeros((120, DEVICES), F32)], axis=0)
    col_form = jnp.transpose(padded)

    for which, table_ref in enumerate((a_ref, b_ref, c_ref, d_ref)):
        fold, rows = FOLD[which], ROWS[which]
        deep = rows // fold
        width = 256 // fold
        for rank in range(2):
            row = col_form[:, rank * 4 + which : rank * 4 + which + 1].astype(I32)
            block = row // deep
            inner = row - block * deep
            acc = jnp.zeros((DEVICES, 256), F32)
            tile = 1024
            for at in range(0, deep, tile):
                index = lax.broadcasted_iota(I32, (DEVICES, tile), 1) + at
                hot = (inner == index).astype(BF16)
                if which < 2:
                    piece = jnp.concatenate(
                        [table_ref[:, q * deep + at : q * deep + at + tile] for q in range(fold)],
                        axis=0,
                    )
                    acc = acc + dot(hot, piece, 1, 1)
                else:
                    piece = jnp.concatenate(
                        [table_ref[q * deep + at : q * deep + at + tile, :] for q in range(fold)],
                        axis=1,
                    )
                    acc = acc + dot(hot, piece)
            value = jnp.zeros((DEVICES, width), F32)
            for q in range(fold):
                value = value + jnp.where(block == q, acc[:, q * width : (q + 1) * width], 0.0)
            at = (0, 64, 256, 512)[which] + rank * (128, 128, 128, 256)[which]
            send_ref[:, at : at + width] = value.astype(BF16)

    pieces, spans = [], []
    for s in range(2):
        hit = targets == 2 * me + s
        pieces.append(jnp.sum(jnp.where(hit, words, 0), axis=0, keepdims=True))
        length = jnp.sum(jnp.where(hit, lengths, 0.0), axis=0, keepdims=True)
        spans.append(jnp.broadcast_to(length, (1, SPAN)))
    event = jnp.concatenate(pieces, axis=1)
    span = jnp.concatenate(spans, axis=1)
    table = event >> TABLE_BITS
    item = event & ((1 << TABLE_BITS) - 1)
    unit = jnp.where(table == 3, item >> 11, jnp.where(table == 2, item >> 11, item >> 12))
    third = jnp.floor((unit.astype(F32) + 0.5) * (1.0 / 3.0)).astype(I32)
    owner = jnp.where(table == 3, unit, third)
    per = jnp.where(table == 3, ROWS[3], jnp.where(table == 2, ROWS[2], ROWS[0]))
    local = item - owner * per
    order = lax.broadcasted_iota(I32, (1, TOKENS), 1)
    key = (local * KEY + order).astype(F32)
    bucket = (table * DEVICES + owner).astype(F32)
    lines = [owner.astype(F32), table.astype(F32), span, key, bucket]
    stacked = jnp.concatenate(lines + [jnp.zeros((123, TOKENS), F32)], axis=0)
    cols = jnp.transpose(stacked)
    ahead = (cols[:, 4:5] == bucket) & (key < cols[:, 3:4])
    rank = jnp.sum(jnp.where(ahead, 1.0, 0.0), axis=1, keepdims=True)
    lane = lax.broadcasted_iota(I32, (TOKENS, 128), 1)
    cols_ref[...] = jnp.where(lane == 3, rank, cols)


def lookup(me, ids, tables):
    return pl.pallas_call(
        lookup_kernel,
        out_shape=(
            jax.ShapeDtypeStruct((DEVICES, 1024), BF16),
            jax.ShapeDtypeStruct((8, DEVICES), F32),
            jax.ShapeDtypeStruct((TOKENS, 128), F32),
        ),
        in_specs=[pl.BlockSpec(memory_space=pltpu.SMEM)] + [VM] * 5,
        out_specs=(VM, VM, VM),
        scratch_shapes=[pltpu.VMEM((SPAN, 512), F32)],
        compiler_params=pltpu.CompilerParams(vmem_limit_bytes=VMEM_LIMIT),
        name="lookup",
    )(me, ids, *tables)


def moments(values):
    mean = jnp.mean(values, axis=-1, keepdims=True)
    centred = values - mean
    scale = lax.rsqrt(jnp.mean(centred * centred, axis=-1, keepdims=True) + 1e-05)
    return centred * scale, scale


def norm_back(grad, normed, scale):
    inner = jnp.mean(grad * normed, axis=-1, keepdims=True)
    return scale * (grad - jnp.mean(grad, axis=-1, keepdims=True) - normed * inner)


def sigmoid(values):
    return 0.5 * jnp.tanh(0.5 * values) + 0.5


def layer_kernel(
    got_ref, cols_ref, w_ref, cot_ref, out_ref, back_ref, g_ref,
    rows_s, emb_s, norm_s, pre_s, act_s, att_s, gated_s, dact_s, datt_s, dpre_s, demb_s, place_s,
):
    half = 128
    proj = w_ref[:, 0:512]
    out_w = w_ref[:, 2560:3072]

    def begin(s, _):
        at = pl.ds(pl.multiple_of(s * SPAN, SPAN), SPAN)
        owner = cols_ref[at, 0:1].astype(I32)
        table = cols_ref[at, 1:2]
        rank = cols_ref[at, 3:4]
        hot = (owner == lax.broadcasted_iota(I32, (SPAN, DEVICES), 1)).astype(BF16)
        lane = lax.broadcasted_iota(I32, (SPAN, half), 1)
        kind = jnp.where(lane < 64, 0.0, 1.0)
        got = dot(hot, got_ref[0])
        first = rank == 0.0
        ab = jnp.where((table == kind), jnp.where(first, got[:, 0:128], got[:, 128:256]), 0.0)
        c = jnp.where(table == 2.0, jnp.where(first, got[:, 256:384], got[:, 384:512]), 0.0)
        got = dot(hot, got_ref[1])
        d = jnp.where(table == 3.0, jnp.where(first, got[:, 0:256], got[:, 256:512]), 0.0)
        rows = jnp.concatenate([ab, c, d], axis=1).astype(BF16)
        rows_s[at, :] = rows
        emb = dot(rows, proj).astype(BF16)
        emb_s[at, :] = emb
        normed, _scale = moments(emb.astype(F32))
        norm_s[at, :] = normed.astype(BF16)
        return 0

    lax.fori_loop(0, 2, begin, 0)

    def project(i, _):
        s, part = i // 4, lax.rem(i, 4)
        at = pl.ds(pl.multiple_of(s * SPAN, SPAN), SPAN)
        lanes = pl.ds(pl.multiple_of(part * 512, 512), 512)
        pre = dot(norm_s[at, :], w_ref[:, pl.ds(pl.multiple_of(part * 512 + 512, 512), 512)])
        pre_s[at, lanes] = pre
        act_s[at, lanes] = (pre * sigmoid(pre)).astype(BF16)
        return 0

    lax.fori_loop(0, 8, project, 0)

    row_id = lax.broadcasted_iota(I32, (SPAN, SPAN), 0)
    col_id = lax.broadcasted_iota(I32, (SPAN, SPAN), 1)

    def head_lanes(kind, head):
        return pl.ds(pl.multiple_of(kind * 512 + head * HEAD, HEAD), HEAD)

    def attend(i, _):
        s, head = i // 4, lax.rem(i, 4)
        at = pl.ds(pl.multiple_of(s * SPAN, SPAN), SPAN)
        keep = (col_id <= row_id) & (col_id.astype(F32) < cols_ref[at, 2:3])
        value = act_s[at, head_lanes(1, head)]
        query = act_s[at, head_lanes(2, head)]
        key = act_s[at, head_lanes(3, head)]
        scores = dot(query, key, 1, 1) * HEAD**-0.5
        attn = jnp.where(keep, scores * sigmoid(scores), 0.0).astype(BF16)
        att_s[at, head_lanes(0, head)] = dot(attn, value)
        return 0

    lax.fori_loop(0, 8, attend, 0)

    def middle(s, _):
        at = pl.ds(pl.multiple_of(s * SPAN, SPAN), SPAN)
        normed, scale = moments(att_s[at, :])
        gate = act_s[at, 0:512].astype(F32)
        gated = (normed * gate).astype(BF16)
        gated_s[at, :] = gated
        branch = dot(gated, out_w)
        out_ref[at, :] = (emb_s[at, :].astype(F32) + branch).astype(BF16)
        where = lax.broadcasted_iota(I32, (SPAN, 1), 0).astype(F32)
        grad = jnp.where(where < cols_ref[at, 2:3], cot_ref[at, :], jnp.zeros((), BF16))
        demb_s[at, :] = grad
        d_gated = dot(grad, out_w, 1, 1).astype(BF16).astype(F32)
        dact_s[at, 0:512] = (d_gated * normed).astype(BF16)
        datt_s[at, :] = norm_back(d_gated * gate, normed, scale).astype(BF16)
        return 0

    lax.fori_loop(0, 2, middle, 0)
    g_ref[:, 2560:3072] = dot(gated_s[...], demb_s[...], 0, 0).astype(BF16)

    def attend_back(i, _):
        s, head = i // 4, lax.rem(i, 4)
        at = pl.ds(pl.multiple_of(s * SPAN, SPAN), SPAN)
        keep = (col_id <= row_id) & (col_id.astype(F32) < cols_ref[at, 2:3])
        value = act_s[at, head_lanes(1, head)]
        query = act_s[at, head_lanes(2, head)]
        key = act_s[at, head_lanes(3, head)]
        d_att = datt_s[at, head_lanes(0, head)]
        scores = dot(query, key, 1, 1) * HEAD**-0.5
        sig = sigmoid(scores)
        attn = jnp.where(keep, scores * sig, 0.0).astype(BF16)
        d_attn = dot(d_att, value, 1, 1).astype(BF16).astype(F32)
        slope = sig * (1.0 + scores * (1.0 - sig))
        d_scores = (jnp.where(keep, d_attn * slope, 0.0) * HEAD**-0.5).astype(BF16)
        dact_s[at, head_lanes(1, head)] = dot(attn, d_att, 0, 0).astype(BF16)
        dact_s[at, head_lanes(2, head)] = dot(d_scores, key).astype(BF16)
        dact_s[at, head_lanes(3, head)] = dot(d_scores, query, 0, 0).astype(BF16)
        return 0

    lax.fori_loop(0, 8, attend_back, 0)

    def project_back(i, _):
        s, part = i // 4, lax.rem(i, 4)
        at = pl.ds(pl.multiple_of(s * SPAN, SPAN), SPAN)
        lanes = pl.ds(pl.multiple_of(part * 512, 512), 512)
        pre = pre_s[at, lanes]
        sig = sigmoid(pre)
        slope = sig * (1.0 + pre * (1.0 - sig))
        dpre_s[at, lanes] = (dact_s[at, lanes].astype(F32) * slope).astype(BF16)
        return 0

    lax.fori_loop(0, 8, project_back, 0)

    def first_weight(part, _):
        lanes = pl.ds(pl.multiple_of(part * 512, 512), 512)
        wide = pl.ds(pl.multiple_of(part * 512 + 512, 512), 512)
        g_ref[:, wide] = dot(norm_s[...], dpre_s[:, lanes], 0, 0).astype(BF16)
        return 0

    lax.fori_loop(0, 4, first_weight, 0)

    def finish(s, _):
        at = pl.ds(pl.multiple_of(s * SPAN, SPAN), SPAN)
        d_normed = dot(dpre_s[at, 0:512], w_ref[:, 512:1024], 1, 1)
        for part in range(1, 4):
            lanes = slice(part * 512, part * 512 + 512)
            wide = slice(part * 512 + 512, part * 512 + 1024)
            d_normed = d_normed + dot(dpre_s[at, lanes], w_ref[:, wide], 1, 1)
        normed, scale = moments(emb_s[at, :].astype(F32))
        back = norm_back(d_normed.astype(BF16).astype(F32), normed, scale)
        d_emb = (demb_s[at, :].astype(F32) + back).astype(BF16)
        demb_s[at, :] = d_emb
        d_rows = dot(d_emb, proj, 1, 1)
        table = cols_ref[at, 1:2]
        rank = cols_ref[at, 3:4]
        lane = lax.broadcasted_iota(I32, (SPAN, half), 1)
        kind = jnp.where(lane < 64, 0.0, 1.0)
        for k in range(2):
            match = rank == float(k)
            low = k * 128
            place_s[at, low : low + 128] = jnp.where(
                (table == kind) & match, d_rows[:, 0:128], 0.0
            ).astype(BF16)
            place_s[at, 256 + low : 384 + low] = jnp.where(
                (table == 2.0) & match, d_rows[:, 128:256], 0.0
            ).astype(BF16)
            low = 512 + k * 256
            place_s[at, low : low + 256] = jnp.where(
                (table == 3.0) & match, d_rows[:, 256:512], 0.0
            ).astype(BF16)
        return 0

    lax.fori_loop(0, 2, finish, 0)
    g_ref[:, 0:512] = dot(rows_s[...], demb_s[...], 0, 0).astype(BF16)
    owner = cols_ref[:, 0:1].astype(I32)
    hot = (owner == lax.broadcasted_iota(I32, (TOKENS, DEVICES), 1)).astype(BF16)
    for part in range(2):
        lanes = slice(part * 512, part * 512 + 512)
        back_ref[:, lanes] = dot(hot, place_s[:, lanes], 0, 0).astype(BF16)


def layer(got, cols, weights, cotangent):
    def vmem(width, kind=BF16):
        return pltpu.VMEM((TOKENS, width), kind)

    return pl.pallas_call(
        layer_kernel,
        out_shape=(
            jax.ShapeDtypeStruct((TOKENS, WIDTH), BF16),
            jax.ShapeDtypeStruct((DEVICES, 1024), BF16),
            jax.ShapeDtypeStruct((512, 3072), BF16),
        ),
        in_specs=[VM] * 4,
        out_specs=(VM, VM, VM),
        scratch_shapes=[
            vmem(512), vmem(512), vmem(512), vmem(2048, F32), vmem(2048), vmem(512, F32),
            vmem(512), vmem(2048), vmem(512), vmem(2048), vmem(512), vmem(1024),
        ],
        compiler_params=pltpu.CompilerParams(vmem_limit_bytes=VMEM_LIMIT),
        name="layer",
    )(got, cols, weights, cotangent)


def scatter_kernel(got_ref, wanted_ref, a_ref, b_ref, c_ref, d_ref):
    row_form = wanted_ref[...]
    padded = jnp.concatenate([row_form, jnp.zeros((120, DEVICES), F32)], axis=0)
    col_form = jnp.transpose(padded)
    for which, out_ref in enumerate((a_ref, b_ref, c_ref, d_ref)):
        fold, rows = FOLD[which], ROWS[which]
        deep = rows // fold
        width = 256 // fold
        spread, inners = [], []
        for rank in range(2):
            row = col_form[:, rank * 4 + which : rank * 4 + which + 1].astype(I32)
            block = row // deep
            at = (0, 64, 256, 512)[which] + rank * (128, 128, 128, 256)[which]
            value = got_ref[:, at : at + width].astype(F32)
            spread.append(
                jnp.concatenate([jnp.where(block == q, value, 0.0) for q in range(fold)], axis=1)
            )
            if which < 2:
                inners.append(row - block * deep)
            else:
                line = row_form[rank * 4 + which : rank * 4 + which + 1].astype(I32)
                inners.append(line - (line // deep) * deep)
        values = jnp.concatenate(spread, axis=0).astype(BF16)
        if which < 2:
            inner = jnp.concatenate(inners, axis=0)
            flipped = jnp.transpose(values.astype(F32)).astype(BF16)
            for at in range(0, deep, 512):
                hot = (inner == lax.broadcasted_iota(I32, (512, 512), 1) + at).astype(BF16)
                summed = dot(flipped, hot).astype(BF16)
                for q in range(fold):
                    out_ref[:, q * deep + at : q * deep + at + 512] = summed[
                        q * width : (q + 1) * width
                    ]
        else:
            inner = jnp.concatenate(inners, axis=1)
            for at in range(0, deep, 512):
                hot = (inner == lax.broadcasted_iota(I32, (512, 512), 0) + at).astype(BF16)
                summed = dot(hot, values).astype(BF16)
                for q in range(fold):
                    out_ref[q * deep + at : q * deep + at + 512, :] = summed[
                        :, q * width : (q + 1) * width
                    ]


def scatter(got, wanted):
    return pl.pallas_call(
        scatter_kernel,
        out_shape=(
            jax.ShapeDtypeStruct((64, ROWS[0]), BF16),
            jax.ShapeDtypeStruct((64, ROWS[1]), BF16),
            jax.ShapeDtypeStruct((ROWS[2], 128), BF16),
            jax.ShapeDtypeStruct((ROWS[3], 256), BF16),
        ),
        in_specs=[VM, VM],
        out_specs=(VM,) * 4,
        compiler_params=pltpu.CompilerParams(vmem_limit_bytes=VMEM_LIMIT),
        name="scatter",
    )(got, wanted)


def reduce_kernel(
    g_ref, proj_ref, in_ref, out_ref,
    across, pair, one, two, line, three, four, parts, column, mine, whole, send_sem, recv_sem,
):
    dp, xy, core, z = place()
    (x, right, left, to_right, to_left), (y, up, down, to_up, to_down) = near()
    along_z, _plane, partner = peers()
    greet(along_z + [to_right, to_left, to_up, to_down] + partner)
    used = [0]

    def start(src, dst, target):
        at = used[0]
        used[0] += 1
        return send(src, dst, send_sem.at[at], recv_sem.at[at], target)

    def finish(copies):
        for copy in copies:
            copy.wait()

    def add(*values):
        total = values[0].astype(F32)
        for value in values[1:]:
            total = total + value.astype(F32)
        return total

    finish([start(g_ref.at[:, :, 1 - core], across, partner[0])])
    far_x, far_y = lax.rem(x + 2, NX), lax.rem(y + 2, NY)

    def merge(k, _):
        i, j = k // NY, lax.rem(k, NY)
        pair[i, j] = add(g_ref[i, j, core], across[i, j]).astype(BF16)
        return 0

    lax.fori_loop(0, PLANE, merge, 0)
    low, high = pl.ds(0, 2), pl.ds(2, 2)
    finish(
        [
            start(pair.at[far_x, low, 0], one.at[0], to_right),
            start(pair.at[far_x, high, 0], one.at[1], to_left),
            start(pair.at[low, far_y, 1], one.at[2], to_up),
            start(pair.at[high, far_y, 1], one.at[3], to_down),
        ]
    )
    for k in range(2):
        pair[right, k, 0] = add(pair[right, k, 0], one[0, k]).astype(BF16)
        pair[left, 2 + k, 0] = add(pair[left, 2 + k, 0], one[1, k]).astype(BF16)
        pair[k, up, 1] = add(pair[k, up, 1], one[2, k]).astype(BF16)
        pair[2 + k, down, 1] = add(pair[2 + k, down, 1], one[3, k]).astype(BF16)
    finish(
        [
            start(pair.at[right, :, 0], two.at[0], to_right),
            start(pair.at[left, :, 0], two.at[1], to_left),
            start(pair.at[:, up, 1], two.at[2], to_up),
            start(pair.at[:, down, 1], two.at[3], to_down),
        ]
    )
    for k in range(4):
        line[0, k] = add(pair[x, k, 0], two[0, k], two[1, k]).astype(BF16)
        line[1, k] = add(pair[k, y, 1], two[2, k], two[3, k]).astype(BF16)
    ahead, behind = pl.ds(0, 1536), pl.ds(1536, 1536)
    finish(
        [
            start(line.at[0, far_y, :, ahead], three.at[0], to_up),
            start(line.at[0, far_y, :, behind], three.at[1], to_down),
            start(line.at[1, far_x, :, ahead], three.at[2], to_right),
            start(line.at[1, far_x, :, behind], three.at[3], to_left),
        ]
    )
    line[0, up, :, ahead] = add(line[0, up, :, ahead], three[0]).astype(BF16)
    line[0, down, :, behind] = add(line[0, down, :, behind], three[1]).astype(BF16)
    line[1, right, :, ahead] = add(line[1, right, :, ahead], three[2]).astype(BF16)
    line[1, left, :, behind] = add(line[1, left, :, behind], three[3]).astype(BF16)
    finish(
        [
            start(line.at[0, up], four.at[0], to_up),
            start(line.at[0, down], four.at[1], to_down),
            start(line.at[1, right], four.at[2], to_right),
            start(line.at[1, left], four.at[3], to_left),
        ]
    )
    for q in range(NZ):
        lanes = pl.ds(q * 384, 384)
        parts[q, 0] = add(line[0, y, :, lanes], four[0, :, lanes], four[1, :, lanes]).astype(BF16)
        parts[q, 1] = add(line[1, x, :, lanes], four[2, :, lanes], four[3, :, lanes]).astype(BF16)
    finish([start(parts.at[t[1]], column.at[i], t) for i, t in enumerate(along_z)])
    mine[...] = add(parts[z], *[column[k] for k in range(NZ - 1)]).astype(BF16)
    copies = [start(mine, whole.at[z], t) for t in along_z]
    whole[pl.ds(z, 1)] = mine[...][None]
    finish(copies)
    for half in range(2):
        rows = slice(half * 8, half * 8 + 8)
        total = jnp.concatenate([whole[q, half].astype(F32) for q in range(NZ)], axis=1)
        proj_ref[rows, :] = total[:, 0:512]
        in_ref[rows, :] = total[:, 512:2560]
        out_ref[rows, :] = total[:, 2560:3072]


def reduce_weights(terms):
    return pl.pallas_call(
        reduce_kernel,
        out_shape=(
            jax.ShapeDtypeStruct((16, 512), F32),
            jax.ShapeDtypeStruct((16, 2048), F32),
            jax.ShapeDtypeStruct((16, 512), F32),
        ),
        in_specs=[VM],
        out_specs=(VM, VM, VM),
        scratch_shapes=[
            pltpu.VMEM((4, 4, 2, 8, 3072), BF16),
            pltpu.VMEM((4, 4, 2, 8, 3072), BF16),
            pltpu.VMEM((4, 2, 8, 3072), BF16),
            pltpu.VMEM((4, 4, 8, 3072), BF16),
            pltpu.VMEM((2, 4, 8, 3072), BF16),
            pltpu.VMEM((4, 8, 1536), BF16),
            pltpu.VMEM((4, 8, 3072), BF16),
            pltpu.VMEM((8, 2, 8, 384), BF16),
            pltpu.VMEM((7, 2, 8, 384), BF16),
            pltpu.VMEM((2, 8, 384), BF16),
            pltpu.VMEM((8, 2, 8, 384), BF16),
            pltpu.SemaphoreType.DMA((31,)),
            pltpu.SemaphoreType.DMA((31,)),
        ],
        compiler_params=pltpu.CompilerParams(
            collective_id=4, has_side_effects=True, vmem_limit_bytes=VMEM_LIMIT
        ),
        name="reduce_weights",
    )(terms)


def shards(
    item_ids, table_ids, lengths, assignment,
    table_a, table_b, table_c, table_d,
    proj_weight, in_weight, out_weight, cotangent,
):
    events = table_ids * (1 << TABLE_BITS) + item_ids
    last = jnp.concatenate(
        [lengths[:, None], assignment[:, None], jnp.zeros((2, 126), I32)], axis=1
    )
    words = jnp.concatenate([events, last], axis=1).reshape(8, 128)
    weights = jnp.concatenate([proj_weight, in_weight, out_weight], axis=1)
    ids, full = share(words, weights.reshape(2, 8, 3072))
    me = (lax.axis_index("dp") * NZ + lax.axis_index("table")).astype(I32).reshape(1)
    outgoing, wanted, cols = lookup(
        me, ids.reshape(DEVICES, 8, 128), (table_a.T, table_b.T, table_c, table_d)
    )
    got = swap(outgoing).reshape(2, DEVICES, 512)
    output, back, terms = layer(
        got, cols, full.reshape(512, 3072), cotangent.reshape(TOKENS, WIDTH)
    )
    arrived = lax.all_to_all(back, ("dp", "table"), 0, 0, tiled=True)
    totals = reduce_weights(terms.reshape(NX, NY, 2, 2, 8, 3072))
    grad_a, grad_b, grad_c, grad_d = scatter(arrived, wanted)
    return (
        output.reshape(2, SPAN, WIDTH),
        grad_a.T,
        grad_b.T,
        grad_c,
        grad_d,
        *totals,
    )


def solution(mesh):
    both = ("dp", "table")
    return jax.shard_map(
        shards,
        mesh=mesh,
        in_specs=(
            P(both, None), P(both, None), P(both), P(both),
            P(both, None), P(both, None), P(both, None), P(both, None),
            P("dp", None), P("dp", None), P("dp", None), P(both, None, None),
        ),
        out_specs=(
            P(both, None, None),
            P(both, None), P(both, None), P(both, None), P(both, None),
            P("dp", None), P("dp", None), P("dp", None),
        ),
        check_vma=False,
    )
```

profile of v0, /device:TPU:8, one launch (start us, length us, event | category | flops | bytes accessed | tf_op | source)
XLA Modules:
  0.0 171.1 jit_solution(5241125506862185864)
XLA Ops:
  0.6 0.7 copy.25
  1.4 0.7 copy.26
  2.1 0.1 pad.6.clone
  2.2 0.7 multiply_add_fusion
  2.9 0.1 add_add_fusion
  3.0 0.6 reshape.46.x_ref
  3.6 1.5 maximum_bitcast_fusion.w_ref
  5.1 34.5 %share.1 = (s32[4,4,2,8,8,128]{5,4,3,2,1,0:T(8,128)}, bf16[4,4,2,2,8,3072]{5,4,3,2,1,0:T(8,128)(2,1)}) custom-call(s32[8,128]{1,0:T(8,128)} %reshape.46.x_ref, bf16[2,8,3072]{2,1,0:T(8,128)(2,1)} %maximum_bitcast_fusion.w_ref), custom_call_target="tpu_custom_call" | custom-call | tf_op jit(solution)/shard_map/share/pallas_call | solution.py:177
  39.6 10.2 %lookup.1 = (bf16[256,1024]{1,0:T(8,128)(2,1)}, f32[8,256]{1,0:T(8,128)}, f32[768,128]{1,0:T(8,128)}) custom-call(s32[1]{0:T(128)} %bitcast.me_ref, s32[256,8,128]{2,1,0:T(8,128)} %bitcast.25, bf16[64,12288]{1,0:T(8,128)(2,1)} %bitcast.23, bf16[64,12288]{1,0:T(8,128)(2,1)} %bitcast.24, bf16[6144,128]{1,0:T(8,128)(2,1)} %c_ref.1, bf16[2048,256]{1,0:T(8,128)(2,1)} %d_ref.1), custom_call_target="tpu_custom_call" | custom-call | tf_op jit(solution)/shard_map/lookup/pallas_call | solution.py:380
  49.9 22.8 %swap.1 = bf16[2,32,8,512]{3,2,1,0:T(8,128)(2,1)} custom-call(bf16[256,1024]{1,0:T(8,128)(2,1)} %get-tuple-element.24.x_ref), custom_call_target="tpu_custom_call" | custom-call | tf_op jit(solution)/shard_map/swap/pallas_call | solution.py:247
  72.7 31.4 %layer.1 = (bf16[768,512]{1,0:T(8,128)(2,1)}, bf16[256,1024]{1,0:T(8,128)(2,1)}, bf16[512,3072]{1,0:T(8,128)(2,1)}) custom-call(bf16[2,256,512]{2,1,0:T(8,128)(2,1)} %bitcast.21, f32[768,128]{1,0:T(8,128)} %get-tuple-element.25.cols_ref, bf16[512,3072]{1,0:T(8,128)(2,1)} %bitcast.20, bf16[768,512]{1,0:T(8,128)(2,1)} %bitcast.26), custom_call_target="tpu_custom_call" | custom-call | tf_op jit(solution)/shard_map/layer/pallas_call | solution.py:578
  104.1 0.5 broadcast.2
  104.6 2.0 %reduce = bf16[256,1024]{1,0:T(8,128)(2,1)S(1)} reduce(bf16[256,1,1024]{2,0,1:T(8,128)(2,1)} %bitcast.27, bf16[]{:T(256)} %broadcast.2), dimensions={1}, to_apply=%copy.27.reduce_sub_computation | reduce | bytes 1048578 | tf_op jit(solution)/shard_map/all_to_all | solution.py:805
  106.6 1.2 reshape.54
  107.8 8.8 %all-to-all-start = ((bf16[256,2,512]{2,1,0:T(2,128)(2,1)}), bf16[256,2,512]{2,1,0:T(2,128)(2,1)S(1)}, u32[]{:S(2)}, u32[]{:S(2)}) async-start(bf16[256,2,512]{2,1,0:T(2,128)(2,1)} %reshape.54), calls=%async_computation | async-start | bytes 1048576 | tf_op jit(solution)/shard_map/all_to_all | solution.py:805
  116.6 45.1 %reduce_weights.1 = (f32[16,512]{1,0:T(8,128)}, f32[16,2048]{1,0:T(8,128)}, f32[16,512]{1,0:T(8,128)}) custom-call(bf16[4,4,2,2,8,3072]{5,4,3,2,1,0:T(8,128)(2,1)} %bitcast.19), custom_call_target="tpu_custom_call" | custom-call | tf_op jit(solution)/shard_map/reduce_weights/pallas_call | solution.py:754
  161.7 0.0 copy-start.2
  161.7 0.0 copy-start
  161.7 0.0 all-to-all-done
  161.7 0.5 reshape.55
  162.2 0.0 copy-start.1
  162.2 1.0 copy.30
  163.1 6.1 %scatter.1 = (bf16[64,12288]{1,0:T(8,128)(2,1)}, bf16[64,12288]{1,0:T(8,128)(2,1)}, bf16[6144,128]{1,0:T(8,128)(2,1)}, bf16[2048,256]{1,0:T(8,128)(2,1)}) custom-call(bf16[256,1024]{1,0:T(8,128)(2,1)} %bitcast.22, f32[8,256]{1,0:T(8,128)} %get-tuple-element.29.wanted_ref), custom_call_target="tpu_custom_call" | custom-call | tf_op jit(solution)/shard_map/scatter/pallas_call | solution.py:641
  169.2 0.0 copy-done.2
  169.3 0.6 copy.35
  169.9 0.0 copy-done
  169.9 0.7 copy.36
  170.5 0.0 copy-done.1
  170.5 0.6 copy.37
  (1 shorter events, 0.0 us)
Async XLA Ops:
  107.8 53.9 %all-to-all-start = ((bf16[256,2,512]{2,1,0:T(2,128)(2,1)}), bf16[256,2,512]{2,1,0:T(2,128)(2,1)S(1)}, u32[]{:S(2)}, u32[]{:S(2)}) async-start(bf16[256,2,512]{2,1,0:T(2,128)(2,1)} %reshape.54), calls=%async_computation | async-start | bytes 1048576 | tf_op jit(solution)/shard_map/all_to_all | solution.py:805
  161.7 7.6 %copy-start.2 = (f32[16,512]{1,0:T(8,128)S(1)}, f32[16,512]{1,0:T(8,128)}, u32[]{:S(2)}) copy-start(f32[16,512]{1,0:T(8,128)} %get-tuple-element.51) | copy-start | bytes 98308
  161.7 8.2 %copy-start = (f32[16,2048]{1,0:T(8,128)S(1)}, f32[16,2048]{1,0:T(8,128)}, u32[]{:S(2)}) copy-start(f32[16,2048]{1,0:T(8,128)} %get-tuple-element.52) | copy-start | bytes 393220
  162.2 8.4 %copy-start.1 = (f32[16,512]{1,0:T(8,128)S(1)}, f32[16,512]{1,0:T(8,128)}, u32[]{:S(2)}) copy-start(f32[16,512]{1,0:T(8,128)} %get-tuple-element.53) | copy-start | bytes 98308
where the time goes:
time: 172 us; the launch traced here: 171 us
  Pallas kernels  150 us (87%)
  starting transfers between devices  8.77 us (5%)
  local copies, waits for them, and re-layouts  7.15 us (4%)
  other arithmetic  4.31 us (3%)
    pallas_call x1, Pallas kernels, reduce_weights(): pl.pallas_call(reduce_kernel, out_shape=(jax.ShapeDtypeStruct((16, 512),...  45.1 us
    pallas_call x1, Pallas kernels, share(): pl.pallas_call(share_kernel, out_shape=(jax.ShapeDtypeStruct((NX, NY, 2,...  34.5 us
    pallas_call x1, Pallas kernels, layer(): pl.pallas_call(layer_kernel, out_shape=(jax.ShapeDtypeStruct((TOKENS, WID...  31.4 us
    pallas_call x1, Pallas kernels, swap(): pl.pallas_call(swap_kernel, out_shape=jax.ShapeDtypeStruct((2, 32, 8, 512...  22.8 us
    pallas_call x1, Pallas kernels, lookup(): pl.pallas_call(lookup_kernel, out_shape=(jax.ShapeDtypeStruct((DEVICES, 1...  10.2 us
    all_to_all x1, starting transfers between devices, shards(): arrived = lax.all_to_all(back, ('dp', 'table'), 0, 0, tiled=True)  8.77 us
    pallas_call x1, Pallas kernels, scatter(): pl.pallas_call(scatter_kernel, out_shape=(jax.ShapeDtypeStruct((64, ROWS[...  6.13 us
    unnamed x12, local copies, waits for them, and re-layouts  4.48 us
  transfers between devices with their start and end apart: 1, of which 0 were waited for; matrix products, arithmetic and copies ran while one was open for 0% of the time, Pallas kernels for 26%

commit v1 on v0

v1 whole, which is shorter than its diff:
```python
import functools

import jax
import jax.numpy as jnp
from jax import lax
from jax.experimental import pallas as pl
from jax.experimental.pallas import tpu as pltpu
from jax.sharding import PartitionSpec as P

MESH = pl.DeviceIdType.MESH
VM = pl.BlockSpec(memory_space=pltpu.VMEM)
F32, BF16, I32 = jnp.float32, jnp.bfloat16, jnp.int32
NX, NY, NZ, PLANE = 4, 4, 8, 16
DEVICES = 256
HEADS, HEAD = 4, 128
SPAN, TOKENS, WIDTH = 384, 768, 512
ROWS = (12288, 12288, 6144, 2048)
FOLD = (4, 4, 2, 1)
TABLE_BITS = 22
KEY = 1024
NONE = 16383.0 * KEY
VMEM_LIMIT = 60 << 20
UNROLL = 2
ANY = pl.BlockSpec(memory_space=pl.ANY)


def place():
    dp, z = lax.axis_index("dp"), lax.axis_index("table")
    return dp, dp // 2, lax.rem(dp, 2), z


def plane_peer(xy, k):
    x = lax.rem(xy // NY + k // NY, NX)
    y = lax.rem(lax.rem(xy, NY) + k % NY, NY)
    return x * NY + y


def peers():
    dp, xy, core, z = place()
    along_z = [(dp, lax.rem(z + k, NZ)) for k in range(1, NZ)]
    in_plane = [(plane_peer(xy, k) * 2 + core, z) for k in range(1, PLANE)]
    return along_z, in_plane, [(xy * 2 + (1 - core), z)]


def near():
    dp, xy, core, z = place()
    x, y = xy // NY, lax.rem(xy, NY)
    right, left = lax.rem(x + 1, NX), lax.rem(x + NX - 1, NX)
    up, down = lax.rem(y + 1, NY), lax.rem(y + NY - 1, NY)

    def at(px, py):
        return ((px * NY + py) * 2 + core, z)

    return (x, right, left, at(right, y), at(left, y)), (y, up, down, at(x, up), at(x, down))


def greet(targets):
    barrier = pltpu.get_barrier_semaphore()
    for dp, z in targets:
        pl.semaphore_signal(barrier, inc=1, device_id=(dp, z), device_id_type=MESH)
    pl.semaphore_wait(barrier, len(targets))


def send(src, dst, send_sem, recv_sem, target):
    copy = pltpu.make_async_remote_copy(
        src_ref=src,
        dst_ref=dst,
        send_sem=send_sem,
        recv_sem=recv_sem,
        device_id=target,
        device_id_type=MESH,
    )
    copy.start()
    return copy


def dot(a, b, da=1, db=0):
    return lax.dot_general(a, b, (((da,), (db,)), ((), ())), preferred_element_type=F32)


class Sender:
    def __init__(self, send_sem, recv_sem):
        self.sems, self.used = (send_sem, recv_sem), 0

    def start(self, src, dst, target):
        at, self.used = self.used, self.used + 1
        return send(src, dst, self.sems[0].at[at], self.sems[1].at[at], target)

    def move(self, ref, target):
        return self.start(ref, ref, target)


def finish(copies):
    for copy in copies:
        copy.wait()


EVERY, LOW, HIGH = slice(None), pl.ds(0, 2), pl.ds(2, 2)
AHEAD, BEHIND = pl.ds(0, 1536), pl.ds(1536, 1536)


def share_kernel(
    items_ref, tables_ref, lengths_ref, targets_ref, proj_ref, in_ref, wout_ref,
    ids_ref, full_ref, send_sem, recv_sem,
):
    dp, xy, core, z = place()
    (x, right, left, to_right, to_left), (y, up, down, to_up, to_down) = near()
    far_x, far_y = lax.rem(x + 2, NX), lax.rem(y + 2, NY)
    to_far_x, to_far_y = ((far_x * NY + y) * 2 + core, z), ((x * NY + far_y) * 2 + core, z)
    lane = lax.broadcasted_iota(I32, (1, 128), 1)
    events = tables_ref[...] * (1 << TABLE_BITS) + items_ref[...]
    lines = []
    for s in range(2):
        lines += [events[s : s + 1, r * 128 : r * 128 + 128] for r in range(3)]
        lines.append(jnp.where(lane == 0, lengths_ref[s], jnp.where(lane == 1, targets_ref[s], 0)))
    ids_ref[x, y, core, z] = jnp.concatenate(lines, axis=0)
    for half in range(2):
        rows = slice(half * 8, half * 8 + 8)
        full_ref[x, y, core, half, :, 0:512] = proj_ref[rows, :]
        full_ref[x, y, core, half, :, 512:2560] = in_ref[rows, :]
        full_ref[x, y, core, half, :, 2560:3072] = wout_ref[rows, :]
    along_z, _plane, partner = peers()
    partner = partner[0]
    near_x, near_y = [to_right, to_left], [to_up, to_down]
    greet(along_z + near_x + near_y + [to_far_x, to_far_y, partner])
    link = Sender(send_sem, recv_sem)

    def ids(px, py, low):
        return ids_ref.at[px, py, core, pl.ds(low, 4)]

    def w(px, py, part):
        return full_ref.at[px, py, core, part]

    own = ids_ref.at[x, y, core, z]
    one = [link.move(own, t) for t in along_z]
    w_one = [link.move(w(x, y, 0), t) for t in near_y] + [link.move(w(x, y, 1), t) for t in near_x]
    finish(one)
    two = [link.move(ids(x, y, 0), t) for t in near_y + [to_far_y]]
    two += [link.move(ids(x, y, 4), t) for t in near_x + [to_far_x]]
    finish(w_one)
    w_two = [
        link.move(full_ref.at[x, down, core, 0, :, AHEAD], to_up),
        link.move(full_ref.at[x, up, core, 0, :, BEHIND], to_down),
        link.move(full_ref.at[left, y, core, 1, :, AHEAD], to_right),
        link.move(full_ref.at[right, y, core, 1, :, BEHIND], to_left),
    ]
    finish(two)
    three = [link.move(ids(x, EVERY, 0), t) for t in [to_far_x] + near_x]
    three += [link.move(ids(EVERY, y, 4), t) for t in [to_far_y] + near_y]
    across = [link.move(ids(x, EVERY, 0), partner), link.move(ids(EVERY, y, 4), partner)]
    finish(w_two)
    w_three = [
        link.move(w(x, EVERY, 0), to_right),
        link.move(w(x, EVERY, 0), to_left),
        link.move(w(EVERY, y, 1), to_up),
        link.move(w(EVERY, y, 1), to_down),
    ]
    across += [link.move(w(x, EVERY, 0), partner), link.move(w(EVERY, y, 1), partner)]
    finish(three)
    across += [link.move(ids(side, EVERY, 0), partner) for side in (right, left, far_x)]
    across += [link.move(ids(EVERY, side, 4), partner) for side in (up, down, far_y)]
    finish(w_three)
    w_four = [
        link.move(w(left, LOW, 0), to_right),
        link.move(w(right, HIGH, 0), to_left),
        link.move(w(LOW, down, 1), to_up),
        link.move(w(HIGH, up, 1), to_down),
    ]
    across += [link.move(w(side, EVERY, 0), partner) for side in (right, left)]
    across += [link.move(w(EVERY, side, 1), partner) for side in (up, down)]
    finish(w_four)
    across += [link.move(w(far_x, EVERY, 0), partner), link.move(w(EVERY, far_y, 1), partner)]
    finish(across)


def sems(count):
    return [pltpu.SemaphoreType.DMA((count,)), pltpu.SemaphoreType.DMA((count,))]


def comm_params(collective):
    return pltpu.CompilerParams(
        collective_id=collective, has_side_effects=True, vmem_limit_bytes=VMEM_LIMIT
    )


SM = pl.BlockSpec(memory_space=pltpu.SMEM)


def share(items, tables, lengths, targets, weights):
    return pl.pallas_call(
        share_kernel,
        out_shape=(
            jax.ShapeDtypeStruct((NX, NY, 2, NZ, 8, 128), I32),
            jax.ShapeDtypeStruct((NX, NY, 2, 2, 8, 3072), BF16),
        ),
        in_specs=[VM, VM, SM, SM, VM, VM, VM],
        out_specs=(VM, VM),
        scratch_shapes=sems(51),
        compiler_params=comm_params(1),
        name="share",
    )(items, tables, lengths, targets, *weights)


class Swap:
    def __init__(self, link, first_ref, second_ref, out_ref, by_z, from_z, by_dp, from_dp, again_z, from_z2):
        self.link, self.first, self.second, self.out = link, first_ref, second_ref, out_ref
        self.by_z, self.from_z, self.by_dp = by_z, from_z, by_dp
        self.from_dp, self.again_z, self.from_z2 = from_dp, again_z, from_z2
        self.dp, xy, core, self.z = place()
        self.along_z, in_plane, partner = peers()
        others = [(plane_peer(xy, k) * 2 + (1 - core), self.z) for k in range(1, PLANE)]
        self.along_dp = in_plane + partner + others
        i = lax.broadcasted_iota(I32, (DEVICES, DEVICES), 0)
        j = lax.broadcasted_iota(I32, (DEVICES, DEVICES), 1)
        self.z_first = (j == (i & 31) * 8 + (i >> 5)).astype(BF16)
        self.dp_first = (j == (i & 7) * 32 + (i >> 3)).astype(BF16)
        by_z[...] = self.arrange(self.z_first, first_ref, (NZ, 32, 512))
        from_z[pl.ds(self.z, 1)] = by_z[pl.ds(self.z, 1)]
        from_dp[pl.ds(self.dp, 1)] = second_ref[pl.ds(self.dp, 1)]

    def arrange(self, matrix, ref, dims):
        return dot(matrix, ref[...].reshape(DEVICES, 512)).astype(BF16).reshape(dims)

    def begin_high(self):
        return [self.link.start(self.by_z.at[t[1]], self.from_z.at[self.z], t) for t in self.along_z]

    def begin_low(self):
        return [
            self.link.start(self.second.at[t[0]], self.from_dp.at[self.dp], t)
            for t in self.along_dp
        ]

    def turn_low(self):
        self.again_z[...] = self.arrange(self.z_first, self.from_dp, (NZ, 32, 512))
        self.from_z2[pl.ds(self.z, 1)] = self.again_z[pl.ds(self.z, 1)]
        return [
            self.link.start(self.again_z.at[t[1]], self.from_z2.at[self.z], t)
            for t in self.along_z
        ]

    def turn_high(self):
        self.by_dp[...] = self.arrange(self.dp_first, self.from_z, (32, NZ, 512))
        self.out[0, pl.ds(self.dp, 1)] = self.by_dp[pl.ds(self.dp, 1)]
        return [
            self.link.start(self.by_dp.at[t[0]], self.out.at[0, self.dp], t) for t in self.along_dp
        ]

    def end_low(self):
        self.out[1] = self.arrange(self.dp_first, self.from_z2, (32, NZ, 512))


SWAP_SHAPES = [
    pltpu.VMEM((8, 32, 512), BF16),
    pltpu.VMEM((8, 32, 512), BF16),
    pltpu.VMEM((32, 8, 512), BF16),
    pltpu.VMEM((32, 8, 512), BF16),
    pltpu.VMEM((8, 32, 512), BF16),
    pltpu.VMEM((8, 32, 512), BF16),
]


def fetch_kernel(first_ref, second_ref, out_ref, *scratch):
    swap = Swap(Sender(*scratch[-2:]), first_ref, second_ref, out_ref, *scratch[:-2])
    greet(swap.along_z + swap.along_dp)
    low, high = swap.begin_low(), swap.begin_high()
    finish(low)
    low = swap.turn_low()
    finish(high)
    high = swap.turn_high()
    finish(low)
    swap.end_low()
    finish(high)


def fetch(first, second):
    return pl.pallas_call(
        fetch_kernel,
        out_shape=jax.ShapeDtypeStruct((2, 32, 8, 512), BF16),
        in_specs=[VM] * 2,
        out_specs=VM,
        scratch_shapes=SWAP_SHAPES + sems(76),
        compiler_params=comm_params(2),
        name="fetch",
    )(first, second)


def smallest_two(keys):
    first = jnp.full((8, keys.shape[1]), NONE, F32)
    second = first
    for at in range(0, keys.shape[0], 8):
        value = keys[at : at + 8]
        second = jnp.minimum(second, jnp.maximum(first, value))
        first = jnp.minimum(first, value)
    low = jnp.min(first, axis=0, keepdims=True)
    high = jnp.min(jnp.where(first == low, second, first), axis=0, keepdims=True)
    return low, high


def lookup_kernel(
    me_ref, ids_ref, a_hbm, b_hbm, c_hbm, d_hbm, first_ref, second_ref, wanted_ref, cols_ref,
    moved, a_ref, b_ref, c_ref, d_ref, sem,
):
    hbm, tables = (a_hbm, b_hbm, c_hbm, d_hbm), (a_ref, b_ref, c_ref, d_ref)
    loads = [pltpu.make_async_copy(hbm[i], tables[i], sem.at[i]) for i in range(4)]
    for copy in loads:
        copy.start()
    me = me_ref[0]
    words = jnp.concatenate(
        [
            jnp.concatenate([ids_ref[:, 4 * s + r, :] for r in range(3)], axis=1)
            for s in range(2)
        ],
        axis=0,
    )
    extra = jnp.concatenate([ids_ref[:, 3, :], ids_ref[:, 7, :]], axis=0)
    lengths = extra[:, 0:1].astype(F32)
    targets = extra[:, 1:2]
    arranged = (targets & 1) * DEVICES + (targets >> 1)
    slots = lax.broadcasted_iota(I32, (512, 512), 1)
    goes = (arranged == slots).astype(BF16)
    total = None
    for shift in (16, 8, 0):
        part = ((words >> shift) & 255).astype(F32).astype(BF16)
        piece = dot(part, goes, 0, 0)
        total = piece if total is None else total * 256.0 + piece
    moved[...] = total

    place_of = lax.broadcasted_iota(I32, (SPAN, 512), 0).astype(F32)
    lows, highs = [], []
    for which in range(4):
        start = which * (1 << TABLE_BITS) + me * ROWS[which]
        local = moved[...] - start.astype(F32)
        held = (local >= 0.0) & (local < float(ROWS[which]))
        keys = jnp.where(held, local * float(KEY) + place_of, NONE)
        low, high = smallest_two(keys)
        low_a, high_a = low[:, :DEVICES], high[:, :DEVICES]
        low_b, high_b = low[:, DEVICES:] + float(SPAN), high[:, DEVICES:] + float(SPAN)
        lows.append(jnp.minimum(low_a, low_b))
        highs.append(jnp.minimum(jnp.maximum(low_a, low_b), jnp.minimum(high_a, high_b)))
    row_form = jnp.floor(jnp.concatenate(lows + highs, axis=0) * (1.0 / KEY))
    wanted_ref[...] = row_form
    padded = jnp.concatenate([row_form, jnp.zeros((120, DEVICES), F32)], axis=0)
    col_form = jnp.transpose(padded)

    for which, table_ref in enumerate(tables):
        loads[which].wait()
        fold, rows = FOLD[which], ROWS[which]
        deep = rows // fold
        width = 256 // fold
        for rank in range(2):
            row = col_form[:, rank * 4 + which : rank * 4 + which + 1].astype(I32)
            block = row // deep
            inner = row - block * deep
            acc = jnp.zeros((DEVICES, 256), F32)
            tile = 1024
            for at in range(0, deep, tile):
                index = lax.broadcasted_iota(I32, (DEVICES, tile), 1) + at
                hot = (inner == index).astype(BF16)
                if which < 2:
                    piece = jnp.concatenate(
                        [table_ref[:, q * deep + at : q * deep + at + tile] for q in range(fold)],
                        axis=0,
                    )
                    acc = acc + dot(hot, piece, 1, 1)
                else:
                    piece = jnp.concatenate(
                        [table_ref[q * deep + at : q * deep + at + tile, :] for q in range(fold)],
                        axis=1,
                    )
                    acc = acc + dot(hot, piece)
            value = jnp.zeros((DEVICES, width), F32)
            for q in range(fold):
                value = value + jnp.where(block == q, acc[:, q * width : (q + 1) * width], 0.0)
            at = (0, 64, 256, 0)[which] + rank * (128, 128, 128, 256)[which]
            part_ref = second_ref if which == 3 else first_ref
            part_ref[:, at : at + width] = value.astype(BF16)

    pieces, spans = [], []
    for s in range(2):
        hit = targets == 2 * me + s
        pieces.append(jnp.sum(jnp.where(hit, words, 0), axis=0, keepdims=True))
        length = jnp.sum(jnp.where(hit, lengths, 0.0), axis=0, keepdims=True)
        spans.append(jnp.broadcast_to(length, (1, SPAN)))
    event = jnp.concatenate(pieces, axis=1)
    span = jnp.concatenate(spans, axis=1)
    table = event >> TABLE_BITS
    item = event & ((1 << TABLE_BITS) - 1)
    unit = jnp.where(table == 3, item >> 11, jnp.where(table == 2, item >> 11, item >> 12))
    third = jnp.floor((unit.astype(F32) + 0.5) * (1.0 / 3.0)).astype(I32)
    owner = jnp.where(table == 3, unit, third)
    per = jnp.where(table == 3, ROWS[3], jnp.where(table == 2, ROWS[2], ROWS[0]))
    local = item - owner * per
    order = lax.broadcasted_iota(I32, (1, TOKENS), 1)
    key = (local * KEY + order).astype(F32)
    bucket = (table * DEVICES + owner).astype(F32)
    lines = [owner.astype(F32), table.astype(F32), span, key, bucket]
    stacked = jnp.concatenate(lines + [jnp.zeros((123, TOKENS), F32)], axis=0)
    cols = jnp.transpose(stacked)
    ahead = (cols[:, 4:5] == bucket) & (key < cols[:, 3:4])
    rank = jnp.sum(jnp.where(ahead, 1.0, 0.0), axis=1, keepdims=True)
    lane = lax.broadcasted_iota(I32, (TOKENS, 128), 1)
    cols_ref[...] = jnp.where(lane == 3, rank, cols)


def lookup(me, ids, tables):
    return pl.pallas_call(
        lookup_kernel,
        out_shape=(
            jax.ShapeDtypeStruct((DEVICES, 512), BF16),
            jax.ShapeDtypeStruct((DEVICES, 512), BF16),
            jax.ShapeDtypeStruct((8, DEVICES), F32),
            jax.ShapeDtypeStruct((TOKENS, 128), F32),
        ),
        in_specs=[SM, VM] + [ANY] * 4,
        out_specs=(VM,) * 4,
        scratch_shapes=[
            pltpu.VMEM((SPAN, 512), F32),
            pltpu.VMEM((64, ROWS[0]), BF16),
            pltpu.VMEM((64, ROWS[1]), BF16),
            pltpu.VMEM((ROWS[2], 128), BF16),
            pltpu.VMEM((ROWS[3], 256), BF16),
            pltpu.SemaphoreType.DMA((4,)),
        ],
        compiler_params=pltpu.CompilerParams(vmem_limit_bytes=VMEM_LIMIT),
        name="lookup",
    )(me, ids, *tables)


def moments(values):
    mean = jnp.mean(values, axis=-1, keepdims=True)
    centred = values - mean
    scale = lax.rsqrt(jnp.mean(centred * centred, axis=-1, keepdims=True) + 1e-05)
    return centred * scale, scale


def norm_back(grad, normed, scale):
    inner = jnp.mean(grad * normed, axis=-1, keepdims=True)
    return scale * (grad - jnp.mean(grad, axis=-1, keepdims=True) - normed * inner)


def sigmoid(values):
    return 0.5 * jnp.tanh(0.5 * values) + 0.5


def layer_kernel(
    got_ref, cols_ref, w_hbm, cot_hbm, out_hbm, first_ref, second_ref, g_hbm,
    rows_s, emb_s, norm_s, slope_s, act_s, att_s, gated_s, datt_s, dpre_s, demb_s, place_s,
    w_ref, cot_ref, out_ref, g_ref, in_sem, out_sem,
):
    half = 128
    pieces = (slice(0, 512), slice(512, 2560), slice(2560, 3072))
    loads = [
        pltpu.make_async_copy(w_hbm.at[:, part], w_ref.at[:, part], in_sem.at[i])
        for i, part in enumerate(pieces)
    ]
    loads.append(pltpu.make_async_copy(cot_hbm, cot_ref, in_sem.at[3]))
    for copy in loads:
        copy.start()
    stores = [
        pltpu.make_async_copy(g_ref.at[:, part], g_hbm.at[:, part], out_sem.at[i])
        for i, part in enumerate(pieces)
    ]
    stores.append(pltpu.make_async_copy(out_ref, out_hbm, out_sem.at[3]))
    loads[0].wait()
    proj = w_ref[:, 0:512]

    def begin(s, _):
        at = pl.ds(pl.multiple_of(s * SPAN, SPAN), SPAN)
        owner = cols_ref[at, 0:1].astype(I32)
        table = cols_ref[at, 1:2]
        rank = cols_ref[at, 3:4]
        hot = (owner == lax.broadcasted_iota(I32, (SPAN, DEVICES), 1)).astype(BF16)
        lane = lax.broadcasted_iota(I32, (SPAN, half), 1)
        kind = jnp.where(lane < 64, 0.0, 1.0)
        got = dot(hot, got_ref[0])
        first = rank == 0.0
        ab = jnp.where((table == kind), jnp.where(first, got[:, 0:128], got[:, 128:256]), 0.0)
        c = jnp.where(table == 2.0, jnp.where(first, got[:, 256:384], got[:, 384:512]), 0.0)
        got = dot(hot, got_ref[1])
        d = jnp.where(table == 3.0, jnp.where(first, got[:, 0:256], got[:, 256:512]), 0.0)
        rows = jnp.concatenate([ab, c, d], axis=1).astype(BF16)
        rows_s[at, :] = rows
        emb = dot(rows, proj).astype(BF16)
        emb_s[at, :] = emb
        normed, _scale = moments(emb.astype(F32))
        norm_s[at, :] = normed.astype(BF16)
        return 0

    lax.fori_loop(0, 2, begin, 0)

    loads[1].wait()

    def project(i, _):
        s, part = i // 4, lax.rem(i, 4)
        at = pl.ds(pl.multiple_of(s * SPAN, SPAN), SPAN)
        lanes = pl.ds(pl.multiple_of(part * 512, 512), 512)
        pre = dot(norm_s[at, :], w_ref[:, pl.ds(pl.multiple_of(part * 512 + 512, 512), 512)])
        sig = sigmoid(pre)
        act = pre * sig
        slope_s[at, lanes] = sig + act * (1.0 - sig)
        act_s[at, lanes] = act.astype(BF16)
        return 0

    lax.fori_loop(0, 8, project, 0)

    blocks = ((0, 256), (256, 384))

    def head_lanes(kind, head):
        return pl.ds(pl.multiple_of(kind * 512 + head * HEAD, HEAD), HEAD)

    def kept(low, high, length):
        row = lax.broadcasted_iota(I32, (high - low, high), 0) + low
        column = lax.broadcasted_iota(I32, (high - low, high), 1)
        return (column <= row) & (column.astype(F32) < length)

    def attend(i, _):
        s, head = i // 4, lax.rem(i, 4)
        at = pl.ds(pl.multiple_of(s * SPAN, SPAN), SPAN)
        length = cols_ref[at, 2:3]
        value = act_s[at, head_lanes(1, head)]
        query = act_s[at, head_lanes(2, head)]
        key = act_s[at, head_lanes(3, head)]
        results = []
        for low, high in blocks:
            scores = dot(query[low:high], key[:high], 1, 1) * HEAD**-0.5
            keep = kept(low, high, length[low:high])
            attn = jnp.where(keep, scores * sigmoid(scores), 0.0).astype(BF16)
            results.append(dot(attn, value[:high]))
        att_s[at, head_lanes(0, head)] = jnp.concatenate(results, axis=0)
        return 0

    lax.fori_loop(0, 8, attend, 0, unroll=UNROLL)
    loads[2].wait()
    loads[3].wait()
    out_w = w_ref[:, 2560:3072]

    def middle(s, _):
        at = pl.ds(pl.multiple_of(s * SPAN, SPAN), SPAN)
        normed, scale = moments(att_s[at, :])
        gate = act_s[at, 0:512].astype(F32)
        gated = (normed * gate).astype(BF16)
        gated_s[at, :] = gated
        branch = dot(gated, out_w)
        out_ref[at, :] = (emb_s[at, :].astype(F32) + branch).astype(BF16)
        where = lax.broadcasted_iota(I32, (SPAN, 1), 0).astype(F32)
        grad = jnp.where(where < cols_ref[at, 2:3], cot_ref[at, :], jnp.zeros((), BF16))
        demb_s[at, :] = grad
        d_gated = dot(grad, out_w, 1, 1).astype(BF16).astype(F32)
        d_gate = (d_gated * normed).astype(BF16).astype(F32)
        dpre_s[at, 0:512] = (d_gate * slope_s[at, 0:512]).astype(BF16)
        datt_s[at, :] = norm_back(d_gated * gate, normed, scale).astype(BF16)
        return 0

    lax.fori_loop(0, 2, middle, 0)
    stores[3].start()
    g_ref[:, 2560:3072] = dot(gated_s[...], demb_s[...], 0, 0).astype(BF16)
    stores[2].start()

    def attend_back(i, _):
        s, head = i // 4, lax.rem(i, 4)
        at = pl.ds(pl.multiple_of(s * SPAN, SPAN), SPAN)
        length = cols_ref[at, 2:3]
        value = act_s[at, head_lanes(1, head)]
        query = act_s[at, head_lanes(2, head)]
        key = act_s[at, head_lanes(3, head)]
        d_att = datt_s[at, head_lanes(0, head)]
        d_query, d_key, d_value = [], [], []
        for low, high in blocks:
            scores = dot(query[low:high], key[:high], 1, 1) * HEAD**-0.5
            sig = sigmoid(scores)
            act = scores * sig
            keep = kept(low, high, length[low:high])
            attn = jnp.where(keep, act, 0.0).astype(BF16)
            d_attn = dot(d_att[low:high], value[:high], 1, 1).astype(BF16).astype(F32)
            slope = sig + act * (1.0 - sig)
            d_scores = (jnp.where(keep, d_attn * slope, 0.0) * HEAD**-0.5).astype(BF16)
            d_value.append(dot(attn, d_att[low:high], 0, 0))
            d_query.append(dot(d_scores, key[:high]))
            d_key.append(dot(d_scores, query[low:high], 0, 0))

        def whole(parts):
            return jnp.concatenate([parts[0] + parts[1][:256], parts[1][256:]], axis=0)

        grads = (whole(d_value), jnp.concatenate(d_query, axis=0), whole(d_key))
        for kind, grad in enumerate(grads):
            lanes = head_lanes(kind + 1, head)
            rounded = grad.astype(BF16).astype(F32)
            dpre_s[at, lanes] = (rounded * slope_s[at, lanes]).astype(BF16)
        return 0

    lax.fori_loop(0, 8, attend_back, 0, unroll=UNROLL)

    def first_weight(part, _):
        lanes = pl.ds(pl.multiple_of(part * 512, 512), 512)
        wide = pl.ds(pl.multiple_of(part * 512 + 512, 512), 512)
        g_ref[:, wide] = dot(norm_s[...], dpre_s[:, lanes], 0, 0).astype(BF16)
        return 0

    lax.fori_loop(0, 4, first_weight, 0)
    stores[1].start()

    def finish(s, _):
        at = pl.ds(pl.multiple_of(s * SPAN, SPAN), SPAN)
        d_normed = dot(dpre_s[at, 0:512], w_ref[:, 512:1024], 1, 1)
        for part in range(1, 4):
            lanes = slice(part * 512, part * 512 + 512)
            wide = slice(part * 512 + 512, part * 512 + 1024)
            d_normed = d_normed + dot(dpre_s[at, lanes], w_ref[:, wide], 1, 1)
        normed, scale = moments(emb_s[at, :].astype(F32))
        back = norm_back(d_normed.astype(BF16).astype(F32), normed, scale)
        d_emb = (demb_s[at, :].astype(F32) + back).astype(BF16)
        demb_s[at, :] = d_emb
        d_rows = dot(d_emb, proj, 1, 1)
        table = cols_ref[at, 1:2]
        rank = cols_ref[at, 3:4]
        lane = lax.broadcasted_iota(I32, (SPAN, half), 1)
        kind = jnp.where(lane < 64, 0.0, 1.0)
        for k in range(2):
            match = rank == float(k)
            low = k * 128
            place_s[at, low : low + 128] = jnp.where(
                (table == kind) & match, d_rows[:, 0:128], 0.0
            ).astype(BF16)
            place_s[at, 256 + low : 384 + low] = jnp.where(
                (table == 2.0) & match, d_rows[:, 128:256], 0.0
            ).astype(BF16)
            low = 512 + k * 256
            place_s[at, low : low + 256] = jnp.where(
                (table == 3.0) & match, d_rows[:, 256:512], 0.0
            ).astype(BF16)
        return 0

    lax.fori_loop(0, 2, finish, 0)
    g_ref[:, 0:512] = dot(rows_s[...], demb_s[...], 0, 0).astype(BF16)
    stores[0].start()
    owner = cols_ref[:, 0:1].astype(I32)
    hot = (owner == lax.broadcasted_iota(I32, (TOKENS, DEVICES), 1)).astype(BF16)
    first_ref[...] = dot(hot, place_s[:, 0:512], 0, 0).astype(BF16)
    second_ref[...] = dot(hot, place_s[:, 512:1024], 0, 0).astype(BF16)
    for copy in stores:
        copy.wait()


def layer(got, cols, weights, cotangent):
    def vmem(width, kind=BF16):
        return pltpu.VMEM((TOKENS, width), kind)

    return pl.pallas_call(
        layer_kernel,
        out_shape=(
            jax.ShapeDtypeStruct((TOKENS, WIDTH), BF16),
            jax.ShapeDtypeStruct((DEVICES, 512), BF16),
            jax.ShapeDtypeStruct((DEVICES, 512), BF16),
            jax.ShapeDtypeStruct((512, 3072), BF16),
        ),
        in_specs=[VM, VM, ANY, ANY],
        out_specs=(ANY, VM, VM, ANY),
        scratch_shapes=[
            vmem(512), vmem(512), vmem(512), vmem(2048, F32), vmem(2048), vmem(512, F32),
            vmem(512), vmem(512), vmem(2048), vmem(512), vmem(1024),
            pltpu.VMEM((512, 3072), BF16), vmem(512), vmem(512), pltpu.VMEM((512, 3072), BF16),
            pltpu.SemaphoreType.DMA((4,)), pltpu.SemaphoreType.DMA((4,)),
        ],
        compiler_params=pltpu.CompilerParams(vmem_limit_bytes=VMEM_LIMIT),
        name="layer",
    )(got, cols, weights, cotangent)


def scatter_kernel(
    got_ref, wanted_ref, total_ref, a_hbm, b_hbm, c_hbm, d_hbm, proj_ref, in_ref, out_ref,
    a_ref, b_ref, c_ref, d_ref, sem,
):
    stores = []
    proj_ref[...] = total_ref[:, 0:512].astype(F32)
    in_ref[...] = total_ref[:, 512:2560].astype(F32)
    out_ref[...] = total_ref[:, 2560:3072].astype(F32)
    row_form = wanted_ref[...]
    padded = jnp.concatenate([row_form, jnp.zeros((120, DEVICES), F32)], axis=0)
    col_form = jnp.transpose(padded)
    pairs = ((a_ref, a_hbm), (b_ref, b_hbm), (c_ref, c_hbm), (d_ref, d_hbm))
    for which, (grad_ref, grad_hbm) in enumerate(pairs):
        fold, rows = FOLD[which], ROWS[which]
        deep = rows // fold
        width = 256 // fold
        spread, inners = [], []
        for rank in range(2):
            row = col_form[:, rank * 4 + which : rank * 4 + which + 1].astype(I32)
            block = row // deep
            at = (0, 64, 256, 0)[which] + rank * (128, 128, 128, 256)[which]
            value = got_ref[which // 3, :, at : at + width].astype(F32)
            spread.append(
                jnp.concatenate([jnp.where(block == q, value, 0.0) for q in range(fold)], axis=1)
            )
            if which < 2:
                inners.append(row - block * deep)
            else:
                line = row_form[rank * 4 + which : rank * 4 + which + 1].astype(I32)
                inners.append(line - (line // deep) * deep)
        values = jnp.concatenate(spread, axis=0).astype(BF16)
        if which < 2:
            inner = jnp.concatenate(inners, axis=0)
            flipped = jnp.transpose(values.astype(F32)).astype(BF16)
            for at in range(0, deep, 512):
                hot = (inner == lax.broadcasted_iota(I32, (512, 512), 1) + at).astype(BF16)
                summed = dot(flipped, hot).astype(BF16)
                for q in range(fold):
                    grad_ref[:, q * deep + at : q * deep + at + 512] = summed[
                        q * width : (q + 1) * width
                    ]
        else:
            inner = jnp.concatenate(inners, axis=1)
            for at in range(0, deep, 512):
                hot = (inner == lax.broadcasted_iota(I32, (512, 512), 0) + at).astype(BF16)
                summed = dot(hot, values).astype(BF16)
                for q in range(fold):
                    grad_ref[q * deep + at : q * deep + at + 512, :] = summed[
                        :, q * width : (q + 1) * width
                    ]
        copy = pltpu.make_async_copy(grad_ref, grad_hbm, sem.at[which])
        copy.start()
        stores.append(copy)
    for copy in stores:
        copy.wait()


def scatter(got, wanted, totals):
    return pl.pallas_call(
        scatter_kernel,
        out_shape=(
            jax.ShapeDtypeStruct((64, ROWS[0]), BF16),
            jax.ShapeDtypeStruct((64, ROWS[1]), BF16),
            jax.ShapeDtypeStruct((ROWS[2], 128), BF16),
            jax.ShapeDtypeStruct((ROWS[3], 256), BF16),
            jax.ShapeDtypeStruct((16, 512), F32),
            jax.ShapeDtypeStruct((16, 2048), F32),
            jax.ShapeDtypeStruct((16, 512), F32),
        ),
        in_specs=[VM, VM, VM],
        out_specs=(ANY,) * 4 + (VM,) * 3,
        scratch_shapes=[
            pltpu.VMEM((64, ROWS[0]), BF16),
            pltpu.VMEM((64, ROWS[1]), BF16),
            pltpu.VMEM((ROWS[2], 128), BF16),
            pltpu.VMEM((ROWS[3], 256), BF16),
            pltpu.SemaphoreType.DMA((4,)),
        ],
        compiler_params=pltpu.CompilerParams(vmem_limit_bytes=VMEM_LIMIT),
        name="scatter",
    )(got, wanted, totals)


def add(*values):
    total = values[0].astype(F32)
    for value in values[1:]:
        total = total + value.astype(F32)
    return total


def deliver_kernel(
    first_ref, second_ref, g_ref, rows_ref, total_ref,
    across, pair, one, two, line, three, four, parts, column, mine, whole, *scratch,
):
    dp, xy, core, z = place()
    (x, right, left, to_right, to_left), (y, up, down, to_up, to_down) = near()
    far_x, far_y = lax.rem(x + 2, NX), lax.rem(y + 2, NY)
    link = Sender(*scratch[-2:])
    swap = Swap(link, first_ref, second_ref, rows_ref, *scratch[:-2])
    greet(swap.along_z + swap.along_dp)
    partner = peers()[2][0]
    start = link.start

    def meet(px, py, part):
        there = (px, py, 1 - core, part)
        return start(g_ref.at[there], across.at[px, py, part], partner)

    def join(px, py, part):
        for k in range(4):
            qx, qy = (px, k) if py is EVERY else (k, py)
            pair[qx, qy, part] = add(g_ref[qx, qy, core, part], across[qx, qy, part]).astype(BF16)

    far = [meet(far_x, EVERY, 0), meet(EVERY, far_y, 1)]
    high = swap.begin_high()
    sides = [
        meet(right, EVERY, 0), meet(left, EVERY, 0), meet(EVERY, up, 1), meet(EVERY, down, 1)
    ]
    centre = [meet(x, EVERY, 0), meet(EVERY, y, 1)]
    finish(far)
    join(far_x, EVERY, 0)
    join(EVERY, far_y, 1)
    steps = [
        start(pair.at[far_x, LOW, 0], one.at[0], to_right),
        start(pair.at[far_x, HIGH, 0], one.at[1], to_left),
        start(pair.at[LOW, far_y, 1], one.at[2], to_up),
        start(pair.at[HIGH, far_y, 1], one.at[3], to_down),
    ]
    low = swap.begin_low()
    finish(sides)
    join(right, EVERY, 0)
    join(left, EVERY, 0)
    join(EVERY, up, 1)
    join(EVERY, down, 1)
    finish(steps)
    for k in range(2):
        pair[right, k, 0] = add(pair[right, k, 0], one[0, k]).astype(BF16)
        pair[left, 2 + k, 0] = add(pair[left, 2 + k, 0], one[1, k]).astype(BF16)
        pair[k, up, 1] = add(pair[k, up, 1], one[2, k]).astype(BF16)
        pair[2 + k, down, 1] = add(pair[2 + k, down, 1], one[3, k]).astype(BF16)
    steps = [
        start(pair.at[right, :, 0], two.at[0], to_right),
        start(pair.at[left, :, 0], two.at[1], to_left),
        start(pair.at[:, up, 1], two.at[2], to_up),
        start(pair.at[:, down, 1], two.at[3], to_down),
    ]
    finish(low)
    low = swap.turn_low()
    finish(centre)
    join(x, EVERY, 0)
    join(EVERY, y, 1)
    finish(steps)
    for k in range(4):
        line[0, k] = add(pair[x, k, 0], two[0, k], two[1, k]).astype(BF16)
        line[1, k] = add(pair[k, y, 1], two[2, k], two[3, k]).astype(BF16)
    steps = [
        start(line.at[0, far_y, :, AHEAD], three.at[0], to_up),
        start(line.at[0, far_y, :, BEHIND], three.at[1], to_down),
        start(line.at[1, far_x, :, AHEAD], three.at[2], to_right),
        start(line.at[1, far_x, :, BEHIND], three.at[3], to_left),
    ]
    finish(high)
    high = swap.turn_high()
    finish(steps)
    line[0, up, :, AHEAD] = add(line[0, up, :, AHEAD], three[0]).astype(BF16)
    line[0, down, :, BEHIND] = add(line[0, down, :, BEHIND], three[1]).astype(BF16)
    line[1, right, :, AHEAD] = add(line[1, right, :, AHEAD], three[2]).astype(BF16)
    line[1, left, :, BEHIND] = add(line[1, left, :, BEHIND], three[3]).astype(BF16)
    finish(
        [
            start(line.at[0, up], four.at[0], to_up),
            start(line.at[0, down], four.at[1], to_down),
            start(line.at[1, right], four.at[2], to_right),
            start(line.at[1, left], four.at[3], to_left),
        ]
    )
    for q in range(NZ):
        lanes = pl.ds(q * 384, 384)
        parts[q, 0] = add(line[0, y, :, lanes], four[0, :, lanes], four[1, :, lanes]).astype(BF16)
        parts[q, 1] = add(line[1, x, :, lanes], four[2, :, lanes], four[3, :, lanes]).astype(BF16)
    steps = [start(parts.at[t[1]], column.at[i], t) for i, t in enumerate(swap.along_z)]
    finish(low)
    swap.end_low()
    finish(steps)
    mine[...] = add(parts[z], *[column[k] for k in range(NZ - 1)]).astype(BF16)
    steps = [start(mine, whole.at[z], t) for t in swap.along_z]
    whole[pl.ds(z, 1)] = mine[...][None]
    finish(high + steps)
    for half in range(2):
        for q in range(NZ):
            total_ref[half * 8 : half * 8 + 8, q * 384 : q * 384 + 384] = whole[q, half]


def deliver(first, second, terms):
    return pl.pallas_call(
        deliver_kernel,
        out_shape=(
            jax.ShapeDtypeStruct((2, 32, 8, 512), BF16),
            jax.ShapeDtypeStruct((16, 3072), BF16),
        ),
        in_specs=[VM] * 3,
        out_specs=(VM, VM),
        scratch_shapes=[
            pltpu.VMEM((4, 4, 2, 8, 3072), BF16),
            pltpu.VMEM((4, 4, 2, 8, 3072), BF16),
            pltpu.VMEM((4, 2, 8, 3072), BF16),
            pltpu.VMEM((4, 4, 8, 3072), BF16),
            pltpu.VMEM((2, 4, 8, 3072), BF16),
            pltpu.VMEM((4, 8, 1536), BF16),
            pltpu.VMEM((4, 8, 3072), BF16),
            pltpu.VMEM((8, 2, 8, 384), BF16),
            pltpu.VMEM((7, 2, 8, 384), BF16),
            pltpu.VMEM((2, 8, 384), BF16),
            pltpu.VMEM((8, 2, 8, 384), BF16),
        ]
        + SWAP_SHAPES
        + sems(114),
        compiler_params=comm_params(3),
        name="deliver",
    )(first, second, terms)


def shards(
    item_ids, table_ids, lengths, assignment,
    table_a, table_b, table_c, table_d,
    proj_weight, in_weight, out_weight, cotangent,
):
    ids, full = share(
        item_ids, table_ids, lengths, assignment, (proj_weight, in_weight, out_weight)
    )
    me = (lax.axis_index("dp") * NZ + lax.axis_index("table")).astype(I32).reshape(1)
    first, second, wanted, cols = lookup(
        me, ids.reshape(DEVICES, 8, 128), (table_a.T, table_b.T, table_c, table_d)
    )
    got = fetch(first, second.reshape(32, 8, 512))
    output, first, second, terms = layer(
        got.reshape(2, DEVICES, 512),
        cols,
        full.reshape(512, 3072),
        cotangent.reshape(TOKENS, WIDTH),
    )
    arrived, totals = deliver(
        first, second.reshape(32, 8, 512), terms.reshape(NX, NY, 2, 2, 8, 3072)
    )
    grads = scatter(arrived.reshape(2, DEVICES, 512), wanted, totals)
    return (
        output.reshape(2, SPAN, WIDTH),
        grads[0].T,
        grads[1].T,
        *grads[2:],
    )


def solution(mesh):
    both = ("dp", "table")
    return jax.shard_map(
        shards,
        mesh=mesh,
        in_specs=(
            P(both, None), P(both, None), P(both), P(both),
            P(both, None), P(both, None), P(both, None), P(both, None),
            P("dp", None), P("dp", None), P("dp", None), P(both, None, None),
        ),
        out_specs=(
            P(both, None, None),
            P(both, None), P(both, None), P(both, None), P(both, None),
            P("dp", None), P("dp", None), P("dp", None),
        ),
        check_vma=False,
    )
```

time: 172 us -> 145 us (0.84)
  starting transfers between devices: 8.77 us -> 0 us
  local copies, waits for them, and re-layouts: 7.15 us -> 0 us
  Pallas kernels: 150 us -> 144 us
  other arithmetic: 4.31 us -> 0 us
    all_to_all x1 -> x0, starting transfers between devices: 8.77 us -> none  [shards(): arrived = lax.all_to_all(back, ('dp', 'table'), 0, 0, tiled=True)]
    unnamed x12 -> x0, local copies, waits for them, and re-layouts: 4.48 us -> none
    pallas_call x3, Pallas kernels: 78.1 us -> 74.3 us  [the longest x1 40.4 us: deliver(): pl.pallas_call(deliver_kernel, out_shape=(jax.ShapeDtypeStruct((2, 32, 8,...]
    pallas_call x1, Pallas kernels: 31.4 us -> 29.3 us  [layer(): pl.pallas_call(layer_kernel, out_shape=(jax.ShapeDtypeStruct((TOKENS, WID...]
    all_to_all x1 -> x0, other arithmetic: 2.03 us -> none  [shards(): arrived = lax.all_to_all(back, ('dp', 'table'), 0, 0, tiled=True)]
  transfers between devices with their start and end apart: 1 -> 0, of which waited for: 0 -> 0; matrix products, arithmetic and copies ran while one was open for 0% -> 0% of each run, Pallas kernels for 26% -> 0%
where the time goes in v1:
time: 145 us; the launch traced here: 144 us
  Pallas kernels  144 us (99%)
    pallas_call x1, Pallas kernels, deliver(): pl.pallas_call(deliver_kernel, out_shape=(jax.ShapeDtypeStruct((2, 32, 8,...  40.4 us
    pallas_call x1, Pallas kernels, share(): pl.pallas_call(share_kernel, out_shape=(jax.ShapeDtypeStruct((NX, NY, 2,...  33 us
    pallas_call x1, Pallas kernels, layer(): pl.pallas_call(layer_kernel, out_shape=(jax.ShapeDtypeStruct((TOKENS, WID...  29.3 us
    pallas_call x1, Pallas kernels, fetch(): pl.pallas_call(fetch_kernel, out_shape=jax.ShapeDtypeStruct((2, 32, 8, 51...  24.3 us
    pallas_call x1, Pallas kernels, lookup(): pl.pallas_call(lookup_kernel, out_shape=(jax.ShapeDtypeStruct((DEVICES, 5...  9.63 us
    pallas_call x1, Pallas kernels, scatter(): pl.pallas_call(scatter_kernel, out_shape=(jax.ShapeDtypeStruct((64, ROWS[...  6.87 us

profile of v1, /device:TPU:8, one launch (start us, length us, event | category | flops | bytes accessed | tf_op | source)
XLA Modules:
  0.0 144.4 jit_solution(8362031581358308287)
XLA Ops:
  0.6 33.0 %share.1 = (s32[4,4,2,8,8,128]{5,4,3,2,1,0:T(8,128)}, bf16[4,4,2,2,8,3072]{5,4,3,2,1,0:T(8,128)(2,1)}) custom-call(s32[2,384]{1,0:T(2,128)} %items_ref.1, s32[2,384]{1,0:T(2,128)} %tables_ref.1, s32[2]{0:T(128)} %lengths_ref.1, s32[2]{0:T(128)} %targets_ref.1, bf16[16,512]{1,0:T(8,128)(2,1)} %proj_ref.1, bf16[16,2048]{1,0:T(8,128)(2,1)} %in_ref.1, ...), custom_call_target="tpu_custom_call" | custom-call | tf_op jit(solution)/shard_map/share/pallas_call | solution.py:190
  33.7 9.6 %lookup.1 = (bf16[256,512]{1,0:T(8,128)(2,1)}, bf16[256,512]{1,0:T(8,128)(2,1)}, f32[8,256]{1,0:T(8,128)}, f32[768,128]{1,0:T(8,128)}) custom-call(s32[1]{0:T(128)} %bitcast.me_ref, s32[256,8,128]{2,1,0:T(8,128)} %bitcast.19, bf16[64,12288]{1,0:T(8,128)(2,1)} %bitcast.17, bf16[64,12288]{1,0:T(8,128)(2,1)} %bitcast.18, bf16[6144,128]{1,0:T(8,128)(2,1)} %c_hbm.1, ...), custom_call_target="tpu_custom_call" | custom-call | tf_op jit(solution)/shard_map/lookup/pallas_call | solution.py:406
  43.3 24.3 %fetch.1 = bf16[2,32,8,512]{3,2,1,0:T(8,128)(2,1)} custom-call(bf16[256,512]{1,0:T(8,128)(2,1)} %get-tuple-element.28.first_ref, bf16[32,8,512]{2,1,0:T(8,128)(2,1)} %bitcast.23), custom_call_target="tpu_custom_call" | custom-call | tf_op jit(solution)/shard_map/fetch/pallas_call | solution.py:276
  67.6 29.3 %layer.1 = (bf16[768,512]{1,0:T(8,128)(2,1)}, bf16[256,512]{1,0:T(8,128)(2,1)}, bf16[256,512]{1,0:T(8,128)(2,1)}, bf16[512,3072]{1,0:T(8,128)(2,1)}) custom-call(bf16[2,256,512]{2,1,0:T(8,128)(2,1)} %bitcast.16, f32[768,128]{1,0:T(8,128)} %get-tuple-element.30.cols_ref, bf16[512,3072]{1,0:T(8,128)(2,1)} %bitcast.14, bf16[768,512]{1,0:T(8,128)(2,1)} %bitcast.20), custom_call_target="tpu_custom_call" | custom-call | tf_op jit(solution)/shard_map/layer/pallas_call | solution.py:648
  96.9 40.4 %deliver.1 = (bf16[2,32,8,512]{3,2,1,0:T(8,128)(2,1)}, bf16[16,3072]{1,0:T(8,128)(2,1)}) custom-call(bf16[256,512]{1,0:T(8,128)(2,1)} %get-tuple-element.33.first_ref, bf16[32,8,512]{2,1,0:T(8,128)(2,1)} %bitcast.22, bf16[4,4,2,2,8,3072]{5,4,3,2,1,0:T(8,128)(2,1)} %bitcast.15), custom_call_target="tpu_custom_call" | custom-call | tf_op jit(solution)/shard_map/deliver/pallas_call | solution.py:862
  137.3 6.9 %scatter.1 = (bf16[64,12288]{1,0:T(8,128)(2,1)}, bf16[64,12288]{1,0:T(8,128)(2,1)}, bf16[6144,128]{1,0:T(8,128)(2,1)}, bf16[2048,256]{1,0:T(8,128)(2,1)}, f32[16...) custom-call(bf16[2,256,512]{2,1,0:T(8,128)(2,1)} %bitcast.21, f32[8,256]{1,0:T(8,128)} %get-tuple-element.37.wanted_ref, ...), custom_call_target="tpu_custom_call" | custom-call | tf_op jit(solution)/shard_map/scatter/pallas_call | solution.py:727

commit v2 on v1

--- a/solution.py
+++ b/solution.py
@@ -20,7 +20,7 @@
 KEY = 1024
 NONE = 16383.0 * KEY
 VMEM_LIMIT = 60 << 20
-UNROLL = 2
+UNROLL = 4
 ANY = pl.BlockSpec(memory_space=pl.ANY)
 
 
@@ -99,11 +99,106 @@
 AHEAD, BEHIND = pl.ds(0, 1536), pl.ds(1536, 1536)
 
 
-def share_kernel(
+def sems(count):
+    return [pltpu.SemaphoreType.DMA((count,)), pltpu.SemaphoreType.DMA((count,))]
+
+
+def comm_params(collective):
+    return pltpu.CompilerParams(
+        collective_id=collective, has_side_effects=True, vmem_limit_bytes=VMEM_LIMIT
+    )
+
+
+SM = pl.BlockSpec(memory_space=pltpu.SMEM)
+
+
+class Swap:
+    def __init__(self, link, first_ref, second_ref, out_ref, by_z, from_z, by_dp, from_dp, again_z, from_z2):
+        self.link, self.first, self.second, self.out = link, first_ref, second_ref, out_ref
+        self.by_z, self.from_z, self.by_dp = by_z, from_z, by_dp
+        self.from_dp, self.again_z, self.from_z2 = from_dp, again_z, from_z2
+        self.dp, xy, core, self.z = place()
+        self.along_z, in_plane, partner = peers()
+        others = [(plane_peer(xy, k) * 2 + (1 - core), self.z) for k in range(1, PLANE)]
+        self.along_dp = in_plane + partner + others
+        i = lax.broadcasted_iota(I32, (DEVICES, DEVICES), 0)
+        j = lax.broadcasted_iota(I32, (DEVICES, DEVICES), 1)
+        self.z_first = (j == (i & 31) * 8 + (i >> 5)).astype(BF16)
+        self.dp_first = (j == (i & 7) * 32 + (i >> 3)).astype(BF16)
+
+    def ready_high(self):
+        self.by_z[...] = self.arrange(self.z_first, self.first, (NZ, 32, 512))
+        self.from_z[pl.ds(self.z, 1)] = self.by_z[pl.ds(self.z, 1)]
+
+    def ready_low(self):
+        self.from_dp[pl.ds(self.dp, 1)] = self.second[pl.ds(self.dp, 1)]
+
+    def arrange(self, matrix, ref, dims):
+        return dot(matrix, ref[...].reshape(DEVICES, 512)).astype(BF16).reshape(dims)
+
+    def begin_high(self):
+        return [self.link.start(self.by_z.at[t[1]], self.from_z.at[self.z], t) for t in self.along_z]
+
+    def begin_low(self):
+        return [
+            self.link.start(self.second.at[t[0]], self.from_dp.at[self.dp], t)
+            for t in self.along_dp
+        ]
+
+    def turn_low(self):
+        self.again_z[...] = self.arrange(self.z_first, self.from_dp, (NZ, 32, 512))
+        self.from_z2[pl.ds(self.z, 1)] = self.again_z[pl.ds(self.z, 1)]
+        return [
+            self.link.start(self.again_z.at[t[1]], self.from_z2.at[self.z], t)
+            for t in self.along_z
+        ]
+
+    def turn_high(self):
+        self.by_dp[...] = self.arrange(self.dp_first, self.from_z, (32, NZ, 512))
+        self.out[0, pl.ds(self.dp, 1)] = self.by_dp[pl.ds(self.dp, 1)]
+        return [
+            self.link.start(self.by_dp.at[t[0]], self.out.at[0, self.dp], t) for t in self.along_dp
+        ]
+
+    def end_low(self):
+        self.out[1] = self.arrange(self.dp_first, self.from_z2, (32, NZ, 512))
+
+
+SWAP_SHAPES = [
+    pltpu.VMEM((8, 32, 512), BF16),
+    pltpu.VMEM((8, 32, 512), BF16),
+    pltpu.VMEM((32, 8, 512), BF16),
+    pltpu.VMEM((32, 8, 512), BF16),
+    pltpu.VMEM((8, 32, 512), BF16),
+    pltpu.VMEM((8, 32, 512), BF16),
+]
+
+
+def smallest_two(keys):
+    first = jnp.full((8, keys.shape[1]), NONE, F32)
+    second = first
+    for at in range(0, keys.shape[0], 8):
+        value = keys[at : at + 8]
+        second = jnp.minimum(second, jnp.maximum(first, value))
+        first = jnp.minimum(first, value)
+    low = jnp.min(first, axis=0, keepdims=True)
+    high = jnp.min(jnp.where(first == low, second, first), axis=0, keepdims=True)
+    return low, high
+
+
+def front_kernel(
     items_ref, tables_ref, lengths_ref, targets_ref, proj_ref, in_ref, wout_ref,
-    ids_ref, full_ref, send_sem, recv_sem,
+    a_hbm, b_hbm, c_hbm, d_hbm,
+    out_ref, full_ref, wanted_ref, cols_ref,
+    ids_ref, moved, first_ref, second_ref, a_ref, b_ref, c_ref, d_ref, sem, *scratch,
 ):
+    *buffers, send_sem, recv_sem = scratch
+    hbm, tables = (a_hbm, b_hbm, c_hbm, d_hbm), (a_ref, b_ref, c_ref, d_ref)
+    loads = [pltpu.make_async_copy(hbm[i], tables[i], sem.at[i]) for i in range(4)]
+    for copy in loads:
+        copy.start()
     dp, xy, core, z = place()
+    me = dp * NZ + z
     (x, right, left, to_right, to_left), (y, up, down, to_up, to_down) = near()
     far_x, far_y = lax.rem(x + 2, NX), lax.rem(y + 2, NY)
     to_far_x, to_far_y = ((far_x * NY + y) * 2 + core, z), ((x * NY + far_y) * 2 + core, z)
@@ -122,8 +217,9 @@
     along_z, _plane, partner = peers()
     partner = partner[0]
     near_x, near_y = [to_right, to_left], [to_up, to_down]
-    greet(along_z + near_x + near_y + [to_far_x, to_far_y, partner])
     link = Sender(send_sem, recv_sem)
+    swap = Swap(link, first_ref, second_ref, out_ref, *buffers)
+    greet(swap.along_z + swap.along_dp)
 
     def ids(px, py, low):
         return ids_ref.at[px, py, core, pl.ds(low, 4)]
@@ -155,164 +251,23 @@
         link.move(w(EVERY, y, 1), to_up),
         link.move(w(EVERY, y, 1), to_down),
     ]
-    across += [link.move(w(x, EVERY, 0), partner), link.move(w(EVERY, y, 1), partner)]
+    w_across = [link.move(w(x, EVERY, 0), partner), link.move(w(EVERY, y, 1), partner)]
     finish(three)
     across += [link.move(ids(side, EVERY, 0), partner) for side in (right, left, far_x)]
     across += [link.move(ids(EVERY, side, 4), partner) for side in (up, down, far_y)]
-    finish(w_three)
-    w_four = [
-        link.move(w(left, LOW, 0), to_right),
-        link.move(w(right, HIGH, 0), to_left),
-        link.move(w(LOW, down, 1), to_up),
-        link.move(w(HIGH, up, 1), to_down),
-    ]
-    across += [link.move(w(side, EVERY, 0), partner) for side in (right, left)]
-    across += [link.move(w(EVERY, side, 1), partner) for side in (up, down)]
-    finish(w_four)
-    across += [link.move(w(far_x, EVERY, 0), partner), link.move(w(EVERY, far_y, 1), partner)]
     finish(across)
 
-
-def sems(count):
-    return [pltpu.SemaphoreType.DMA((count,)), pltpu.SemaphoreType.DMA((count,))]
-
-
-def comm_params(collective):
-    return pltpu.CompilerParams(
-        collective_id=collective, has_side_effects=True, vmem_limit_bytes=VMEM_LIMIT
-    )
-
-
-SM = pl.BlockSpec(memory_space=pltpu.SMEM)
-
-
-def share(items, tables, lengths, targets, weights):
-    return pl.pallas_call(
-        share_kernel,
-        out_shape=(
-            jax.ShapeDtypeStruct((NX, NY, 2, NZ, 8, 128), I32),
-            jax.ShapeDtypeStruct((NX, NY, 2, 2, 8, 3072), BF16),
-        ),
-        in_specs=[VM, VM, SM, SM, VM, VM, VM],
-        out_specs=(VM, VM),
-        scratch_shapes=sems(51),
-        compiler_params=comm_params(1),
-        name="share",
-    )(items, tables, lengths, targets, *weights)
-
-
-class Swap:
-    def __init__(self, link, first_ref, second_ref, out_ref, by_z, from_z, by_dp, from_dp, again_z, from_z2):
-        self.link, self.first, self.second, self.out = link, first_ref, second_ref, out_ref
-        self.by_z, self.from_z, self.by_dp = by_z, from_z, by_dp
-        self.from_dp, self.again_z, self.from_z2 = from_dp, again_z, from_z2
-        self.dp, xy, core, self.z = place()
-        self.along_z, in_plane, partner = peers()
-        others = [(plane_peer(xy, k) * 2 + (1 - core), self.z) for k in range(1, PLANE)]
-        self.along_dp = in_plane + partner + others
-        i = lax.broadcasted_iota(I32, (DEVICES, DEVICES), 0)
-        j = lax.broadcasted_iota(I32, (DEVICES, DEVICES), 1)
-        self.z_first = (j == (i & 31) * 8 + (i >> 5)).astype(BF16)
-        self.dp_first = (j == (i & 7) * 32 + (i >> 3)).astype(BF16)
-        by_z[...] = self.arrange(self.z_first, first_ref, (NZ, 32, 512))
-        from_z[pl.ds(self.z, 1)] = by_z[pl.ds(self.z, 1)]
-        from_dp[pl.ds(self.dp, 1)] = second_ref[pl.ds(self.dp, 1)]
-
-    def arrange(self, matrix, ref, dims):
-        return dot(matrix, ref[...].reshape(DEVICES, 512)).astype(BF16).reshape(dims)
-
-    def begin_high(self):
-        return [self.link.start(self.by_z.at[t[1]], self.from_z.at[self.z], t) for t in self.along_z]
-
-    def begin_low(self):
-        return [
-            self.link.start(self.second.at[t[0]], self.from_dp.at[self.dp], t)
-            for t in self.along_dp
-        ]
-
-    def turn_low(self):
-        self.again_z[...] = self.arrange(self.z_first, self.from_dp, (NZ, 32, 512))
-        self.from_z2[pl.ds(self.z, 1)] = self.again_z[pl.ds(self.z, 1)]
-        return [
-            self.link.start(self.again_z.at[t[1]], self.from_z2.at[self.z], t)
-            for t in self.along_z
-        ]
-
-    def turn_high(self):
-        self.by_dp[...] = self.arrange(self.dp_first, self.from_z, (32, NZ, 512))
-        self.out[0, pl.ds(self.dp, 1)] = self.by_dp[pl.ds(self.dp, 1)]
-        return [
-            self.link.start(self.by_dp.at[t[0]], self.out.at[0, self.dp], t) for t in self.along_dp
-        ]
-
-    def end_low(self):
-        self.out[1] = self.arrange(self.dp_first, self.from_z2, (32, NZ, 512))
-
-
-SWAP_SHAPES = [
-    pltpu.VMEM((8, 32, 512), BF16),
-    pltpu.VMEM((8, 32, 512), BF16),
-    pltpu.VMEM((32, 8, 512), BF16),
-    pltpu.VMEM((32, 8, 512), BF16),
-    pltpu.VMEM((8, 32, 512), BF16),
-    pltpu.VMEM((8, 32, 512), BF16),
-]
-
-
-def fetch_kernel(first_ref, second_ref, out_ref, *scratch):
-    swap = Swap(Sender(*scratch[-2:]), first_ref, second_ref, out_ref, *scratch[:-2])
-    greet(swap.along_z + swap.along_dp)
-    low, high = swap.begin_low(), swap.begin_high()
-    finish(low)
-    low = swap.turn_low()
-    finish(high)
-    high = swap.turn_high()
-    finish(low)
-    swap.end_low()
-    finish(high)
-
-
-def fetch(first, second):
-    return pl.pallas_call(
-        fetch_kernel,
-        out_shape=jax.ShapeDtypeStruct((2, 32, 8, 512), BF16),
-        in_specs=[VM] * 2,
-        out_specs=VM,
-        scratch_shapes=SWAP_SHAPES + sems(76),
-        compiler_params=comm_params(2),
-        name="fetch",
-    )(first, second)
-
-
-def smallest_two(keys):
-    first = jnp.full((8, keys.shape[1]), NONE, F32)
-    second = first
-    for at in range(0, keys.shape[0], 8):
-        value = keys[at : at + 8]
-        second = jnp.minimum(second, jnp.maximum(first, value))
-        first = jnp.minimum(first, value)
-    low = jnp.min(first, axis=0, keepdims=True)
-    high = jnp.min(jnp.where(first == low, second, first), axis=0, keepdims=True)
-    return low, high
-
-
-def lookup_kernel(
-    me_ref, ids_ref, a_hbm, b_hbm, c_hbm, d_hbm, first_ref, second_ref, wanted_ref, cols_ref,
-    moved, a_ref, b_ref, c_ref, d_ref, sem,
-):
-    hbm, tables = (a_hbm, b_hbm, c_hbm, d_hbm), (a_ref, b_ref, c_ref, d_ref)
-    loads = [pltpu.make_async_copy(hbm[i], tables[i], sem.at[i]) for i in range(4)]
-    for copy in loads:
-        copy.start()
-    me = me_ref[0]
+    def line_of(j):
+        return ids_ref[:, :, :, :, j, :].reshape(DEVICES, 128)
+
     words = jnp.concatenate(
         [
-            jnp.concatenate([ids_ref[:, 4 * s + r, :] for r in range(3)], axis=1)
+            jnp.concatenate([line_of(4 * s + r) for r in range(3)], axis=1)
             for s in range(2)
         ],
         axis=0,
     )
-    extra = jnp.concatenate([ids_ref[:, 3, :], ids_ref[:, 7, :]], axis=0)
+    extra = jnp.concatenate([line_of(3), line_of(7)], axis=0)
     lengths = extra[:, 0:1].astype(F32)
     targets = extra[:, 1:2]
     arranged = (targets & 1) * DEVICES + (targets >> 1)
@@ -342,7 +297,8 @@
     padded = jnp.concatenate([row_form, jnp.zeros((120, DEVICES), F32)], axis=0)
     col_form = jnp.transpose(padded)
 
-    for which, table_ref in enumerate(tables):
+    def find(which):
+        table_ref = tables[which]
         loads[which].wait()
         fold, rows = FOLD[which], ROWS[which]
         deep = rows // fold
@@ -372,8 +328,31 @@
             for q in range(fold):
                 value = value + jnp.where(block == q, acc[:, q * width : (q + 1) * width], 0.0)
             at = (0, 64, 256, 0)[which] + rank * (128, 128, 128, 256)[which]
-            part_ref = second_ref if which == 3 else first_ref
-            part_ref[:, at : at + width] = value.astype(BF16)
+            if which == 3:
+                second_ref[:, :, at : at + width] = value.astype(BF16).reshape(32, NZ, width)
+            else:
+                first_ref[:, at : at + width] = value.astype(BF16)
+
+    find(3)
+    swap.ready_low()
+    low = swap.begin_low()
+    finish(w_three)
+    w_four = [
+        link.move(w(left, LOW, 0), to_right),
+        link.move(w(right, HIGH, 0), to_left),
+        link.move(w(LOW, down, 1), to_up),
+        link.move(w(HIGH, up, 1), to_down),
+    ]
+    w_across += [link.move(w(side, EVERY, 0), partner) for side in (right, left)]
+    w_across += [link.move(w(EVERY, side, 1), partner) for side in (up, down)]
+    for which in range(3):
+        find(which)
+    swap.ready_high()
+    high = swap.begin_high()
+    finish(low)
+    low = swap.turn_low()
+    finish(w_four)
+    w_across += [link.move(w(far_x, EVERY, 0), partner), link.move(w(EVERY, far_y, 1), partner)]
 
     pieces, spans = [], []
     for s in range(2):
@@ -401,29 +380,40 @@
     lane = lax.broadcasted_iota(I32, (TOKENS, 128), 1)
     cols_ref[...] = jnp.where(lane == 3, rank, cols)
 
-
-def lookup(me, ids, tables):
+    finish(high)
+    high = swap.turn_high()
+    finish(low)
+    swap.end_low()
+    finish(high + w_across)
+
+
+def front(items, tables, lengths, targets, weights, held):
     return pl.pallas_call(
-        lookup_kernel,
+        front_kernel,
         out_shape=(
-            jax.ShapeDtypeStruct((DEVICES, 512), BF16),
-            jax.ShapeDtypeStruct((DEVICES, 512), BF16),
+            jax.ShapeDtypeStruct((2, 32, 8, 512), BF16),
+            jax.ShapeDtypeStruct((NX, NY, 2, 2, 8, 3072), BF16),
             jax.ShapeDtypeStruct((8, DEVICES), F32),
             jax.ShapeDtypeStruct((TOKENS, 128), F32),
         ),
-        in_specs=[SM, VM] + [ANY] * 4,
+        in_specs=[VM, VM, SM, SM, VM, VM, VM] + [ANY] * 4,
         out_specs=(VM,) * 4,
         scratch_shapes=[
+            pltpu.VMEM((NX, NY, 2, NZ, 8, 128), I32),
             pltpu.VMEM((SPAN, 512), F32),
+            pltpu.VMEM((DEVICES, 512), BF16),
+            pltpu.VMEM((32, NZ, 512), BF16),
             pltpu.VMEM((64, ROWS[0]), BF16),
             pltpu.VMEM((64, ROWS[1]), BF16),
             pltpu.VMEM((ROWS[2], 128), BF16),
             pltpu.VMEM((ROWS[3], 256), BF16),
             pltpu.SemaphoreType.DMA((4,)),
-        ],
-        compiler_params=pltpu.CompilerParams(vmem_limit_bytes=VMEM_LIMIT),
-        name="lookup",
-    )(me, ids, *tables)
+        ]
+        + SWAP_SHAPES
+        + sems(127),
+        compiler_params=comm_params(1),
+        name="front",
+    )(items, tables, lengths, targets, *weights, *held)
 
 
 def moments(values):
@@ -765,6 +755,8 @@
     far_x, far_y = lax.rem(x + 2, NX), lax.rem(y + 2, NY)
     link = Sender(*scratch[-2:])
     swap = Swap(link, first_ref, second_ref, rows_ref, *scratch[:-2])
+    swap.ready_high()
+    swap.ready_low()
     greet(swap.along_z + swap.along_dp)
     partner = peers()[2][0]
     start = link.start
@@ -892,14 +884,14 @@
     table_a, table_b, table_c, table_d,
     proj_weight, in_weight, out_weight, cotangent,
 ):
-    ids, full = share(
-        item_ids, table_ids, lengths, assignment, (proj_weight, in_weight, out_weight)
+    got, full, wanted, cols = front(
+        item_ids,
+        table_ids,
+        lengths,
+        assignment,
+        (proj_weight, in_weight, out_weight),
+        (table_a.T, table_b.T, table_c, table_d),
     )
-    me = (lax.axis_index("dp") * NZ + lax.axis_index("table")).astype(I32).reshape(1)
-    first, second, wanted, cols = lookup(
-        me, ids.reshape(DEVICES, 8, 128), (table_a.T, table_b.T, table_c, table_d)
-    )
-    got = fetch(first, second.reshape(32, 8, 512))
     output, first, second, terms = layer(
         got.reshape(2, DEVICES, 512),
         cols,

time: 145 us -> 130 us (0.90)
  Pallas kernels: 144 us -> 129 us
    pallas_call x3 -> x1, Pallas kernels: 66.9 us -> 51.4 us  [front(): pl.pallas_call(front_kernel, out_shape=(jax.ShapeDtypeStruct((2, 32, 8, 5...]
    pallas_call x1, Pallas kernels: 40.4 us -> 42.6 us  [deliver(): pl.pallas_call(deliver_kernel, out_shape=(jax.ShapeDtypeStruct((2, 32, 8,...]
where the time goes in v2:
time: 130 us
  Pallas kernels  129 us (99%)
    pallas_call x1, Pallas kernels, front(): pl.pallas_call(front_kernel, out_shape=(jax.ShapeDtypeStruct((2, 32, 8, 5...  51.4 us
    pallas_call x1, Pallas kernels, deliver(): pl.pallas_call(deliver_kernel, out_shape=(jax.ShapeDtypeStruct((2, 32, 8,...  42.6 us
    pallas_call x1, Pallas kernels, layer(): pl.pallas_call(layer_kernel, out_shape=(jax.ShapeDtypeStruct((TOKENS, WID...  28.4 us
    pallas_call x1, Pallas kernels, scatter(): pl.pallas_call(scatter_kernel, out_shape=(jax.ShapeDtypeStruct((64, ROWS[...  6.87 us

profile of v2, /device:TPU:8, one launch (start us, length us, event | category | flops | bytes accessed | tf_op | source)
XLA Modules:
  0.0 130.1 jit_solution(2509543490508236664)
XLA Ops:
  0.6 51.4 %front.1 = (bf16[2,32,8,512]{3,2,1,0:T(8,128)(2,1)}, bf16[4,4,2,2,8,3072]{5,4,3,2,1,0:T(8,128)(2,1)}, f32[8,256]{1,0:T(8,128)}, f32[768,128]{1,0:T(8,128)}) custom-call(s32[2,384]{1,0:T(2,128)} %items_ref.1, s32[2,384]{1,0:T(2,128)} %tables_ref.1, s32[2]{0:T(128)} %lengths_ref.1, s32[2]{0:T(128)} %targets_ref.1, bf16[16,512]{1,0:T(8,128)(2,1)} %proj_ref.1, ...), custom_call_target="tpu_custom_call" | custom-call | tf_op jit(solution)/shard_map/front/pallas_call | solution.py:391
  52.0 28.4 %layer.1 = (bf16[768,512]{1,0:T(8,128)(2,1)}, bf16[256,512]{1,0:T(8,128)(2,1)}, bf16[256,512]{1,0:T(8,128)(2,1)}, bf16[512,3072]{1,0:T(8,128)(2,1)}) custom-call(bf16[2,256,512]{2,1,0:T(8,128)(2,1)} %bitcast.16, f32[768,128]{1,0:T(8,128)} %get-tuple-element.26.cols_ref, bf16[512,3072]{1,0:T(8,128)(2,1)} %bitcast.12, bf16[768,512]{1,0:T(8,128)(2,1)} %bitcast.15), custom_call_target="tpu_custom_call" | custom-call | tf_op jit(solution)/shard_map/layer/pallas_call | solution.py:638
  80.4 42.6 %deliver.1 = (bf16[2,32,8,512]{3,2,1,0:T(8,128)(2,1)}, bf16[16,3072]{1,0:T(8,128)(2,1)}) custom-call(bf16[256,512]{1,0:T(8,128)(2,1)} %get-tuple-element.29.first_ref, bf16[32,8,512]{2,1,0:T(8,128)(2,1)} %bitcast.18, bf16[4,4,2,2,8,3072]{5,4,3,2,1,0:T(8,128)(2,1)} %bitcast.11), custom_call_target="tpu_custom_call" | custom-call | tf_op jit(solution)/shard_map/deliver/pallas_call | solution.py:854
  123.0 6.9 %scatter.1 = (bf16[64,12288]{1,0:T(8,128)(2,1)}, bf16[64,12288]{1,0:T(8,128)(2,1)}, bf16[6144,128]{1,0:T(8,128)(2,1)}, bf16[2048,256]{1,0:T(8,128)(2,1)}, f32[16...) custom-call(bf16[2,256,512]{2,1,0:T(8,128)(2,1)} %bitcast.17, f32[8,256]{1,0:T(8,128)} %get-tuple-element.33.wanted_ref, ...), custom_call_target="tpu_custom_call" | custom-call | tf_op jit(solution)/shard_map/scatter/pallas_call | solution.py:717

commit v3 on v2

--- a/solution.py
+++ b/solution.py
@@ -54,11 +54,19 @@
     return (x, right, left, at(right, y), at(left, y)), (y, up, down, at(x, up), at(x, down))
 
 
-def greet(targets):
+def knock(targets):
     barrier = pltpu.get_barrier_semaphore()
     for dp, z in targets:
         pl.semaphore_signal(barrier, inc=1, device_id=(dp, z), device_id_type=MESH)
-    pl.semaphore_wait(barrier, len(targets))
+
+
+def admit(targets):
+    pl.semaphore_wait(pltpu.get_barrier_semaphore(), len(targets))
+
+
+def greet(targets):
+    knock(targets)
+    admit(targets)
 
 
 def send(src, dst, send_sem, recv_sem, target):
@@ -430,230 +438,6 @@
 
 def sigmoid(values):
     return 0.5 * jnp.tanh(0.5 * values) + 0.5
-
-
-def layer_kernel(
-    got_ref, cols_ref, w_hbm, cot_hbm, out_hbm, first_ref, second_ref, g_hbm,
-    rows_s, emb_s, norm_s, slope_s, act_s, att_s, gated_s, datt_s, dpre_s, demb_s, place_s,
-    w_ref, cot_ref, out_ref, g_ref, in_sem, out_sem,
-):
-    half = 128
-    pieces = (slice(0, 512), slice(512, 2560), slice(2560, 3072))
-    loads = [
-        pltpu.make_async_copy(w_hbm.at[:, part], w_ref.at[:, part], in_sem.at[i])
-        for i, part in enumerate(pieces)
-    ]
-    loads.append(pltpu.make_async_copy(cot_hbm, cot_ref, in_sem.at[3]))
-    for copy in loads:
-        copy.start()
-    stores = [
-        pltpu.make_async_copy(g_ref.at[:, part], g_hbm.at[:, part], out_sem.at[i])
-        for i, part in enumerate(pieces)
-    ]
-    stores.append(pltpu.make_async_copy(out_ref, out_hbm, out_sem.at[3]))
-    loads[0].wait()
-    proj = w_ref[:, 0:512]
-
-    def begin(s, _):
-        at = pl.ds(pl.multiple_of(s * SPAN, SPAN), SPAN)
-        owner = cols_ref[at, 0:1].astype(I32)
-        table = cols_ref[at, 1:2]
-        rank = cols_ref[at, 3:4]
-        hot = (owner == lax.broadcasted_iota(I32, (SPAN, DEVICES), 1)).astype(BF16)
-        lane = lax.broadcasted_iota(I32, (SPAN, half), 1)
-        kind = jnp.where(lane < 64, 0.0, 1.0)
-        got = dot(hot, got_ref[0])
-        first = rank == 0.0
-        ab = jnp.where((table == kind), jnp.where(first, got[:, 0:128], got[:, 128:256]), 0.0)
-        c = jnp.where(table == 2.0, jnp.where(first, got[:, 256:384], got[:, 384:512]), 0.0)
-        got = dot(hot, got_ref[1])
-        d = jnp.where(table == 3.0, jnp.where(first, got[:, 0:256], got[:, 256:512]), 0.0)
-        rows = jnp.concatenate([ab, c, d], axis=1).astype(BF16)
-        rows_s[at, :] = rows
-        emb = dot(rows, proj).astype(BF16)
-        emb_s[at, :] = emb
-        normed, _scale = moments(emb.astype(F32))
-        norm_s[at, :] = normed.astype(BF16)
-        return 0
-
-    lax.fori_loop(0, 2, begin, 0)
-
-    loads[1].wait()
-
-    def project(i, _):
-        s, part = i // 4, lax.rem(i, 4)
-        at = pl.ds(pl.multiple_of(s * SPAN, SPAN), SPAN)
-        lanes = pl.ds(pl.multiple_of(part * 512, 512), 512)
-        pre = dot(norm_s[at, :], w_ref[:, pl.ds(pl.multiple_of(part * 512 + 512, 512), 512)])
-        sig = sigmoid(pre)
-        act = pre * sig
-        slope_s[at, lanes] = sig + act * (1.0 - sig)
-        act_s[at, lanes] = act.astype(BF16)
-        return 0
-
-    lax.fori_loop(0, 8, project, 0)
-
-    blocks = ((0, 256), (256, 384))
-
-    def head_lanes(kind, head):
-        return pl.ds(pl.multiple_of(kind * 512 + head * HEAD, HEAD), HEAD)
-
-    def kept(low, high, length):
-        row = lax.broadcasted_iota(I32, (high - low, high), 0) + low
-        column = lax.broadcasted_iota(I32, (high - low, high), 1)
-        return (column <= row) & (column.astype(F32) < length)
-
-    def attend(i, _):
-        s, head = i // 4, lax.rem(i, 4)
-        at = pl.ds(pl.multiple_of(s * SPAN, SPAN), SPAN)
-        length = cols_ref[at, 2:3]
-        value = act_s[at, head_lanes(1, head)]
-        query = act_s[at, head_lanes(2, head)]
-        key = act_s[at, head_lanes(3, head)]
-        results = []
-        for low, high in blocks:
-            scores = dot(query[low:high], key[:high], 1, 1) * HEAD**-0.5
-            keep = kept(low, high, length[low:high])
-            attn = jnp.where(keep, scores * sigmoid(scores), 0.0).astype(BF16)
-            results.append(dot(attn, value[:high]))
-        att_s[at, head_lanes(0, head)] = jnp.concatenate(results, axis=0)
-        return 0
-
-    lax.fori_loop(0, 8, attend, 0, unroll=UNROLL)
-    loads[2].wait()
-    loads[3].wait()
-    out_w = w_ref[:, 2560:3072]
-
-    def middle(s, _):
-        at = pl.ds(pl.multiple_of(s * SPAN, SPAN), SPAN)
-        normed, scale = moments(att_s[at, :])
-        gate = act_s[at, 0:512].astype(F32)
-        gated = (normed * gate).astype(BF16)
-        gated_s[at, :] = gated
-        branch = dot(gated, out_w)
-        out_ref[at, :] = (emb_s[at, :].astype(F32) + branch).astype(BF16)
-        where = lax.broadcasted_iota(I32, (SPAN, 1), 0).astype(F32)
-        grad = jnp.where(where < cols_ref[at, 2:3], cot_ref[at, :], jnp.zeros((), BF16))
-        demb_s[at, :] = grad
-        d_gated = dot(grad, out_w, 1, 1).astype(BF16).astype(F32)
-        d_gate = (d_gated * normed).astype(BF16).astype(F32)
-        dpre_s[at, 0:512] = (d_gate * slope_s[at, 0:512]).astype(BF16)
-        datt_s[at, :] = norm_back(d_gated * gate, normed, scale).astype(BF16)
-        return 0
-
-    lax.fori_loop(0, 2, middle, 0)
-    stores[3].start()
-    g_ref[:, 2560:3072] = dot(gated_s[...], demb_s[...], 0, 0).astype(BF16)
-    stores[2].start()
-
-    def attend_back(i, _):
-        s, head = i // 4, lax.rem(i, 4)
-        at = pl.ds(pl.multiple_of(s * SPAN, SPAN), SPAN)
-        length = cols_ref[at, 2:3]
-        value = act_s[at, head_lanes(1, head)]
-        query = act_s[at, head_lanes(2, head)]
-        key = act_s[at, head_lanes(3, head)]
-        d_att = datt_s[at, head_lanes(0, head)]
-        d_query, d_key, d_value = [], [], []
-        for low, high in blocks:
-            scores = dot(query[low:high], key[:high], 1, 1) * HEAD**-0.5
-            sig = sigmoid(scores)
-            act = scores * sig
-            keep = kept(low, high, length[low:high])
-            attn = jnp.where(keep, act, 0.0).astype(BF16)
-            d_attn = dot(d_att[low:high], value[:high], 1, 1).astype(BF16).astype(F32)
-            slope = sig + act * (1.0 - sig)
-            d_scores = (jnp.where(keep, d_attn * slope, 0.0) * HEAD**-0.5).astype(BF16)
-            d_value.append(dot(attn, d_att[low:high], 0, 0))
-            d_query.append(dot(d_scores, key[:high]))
-            d_key.append(dot(d_scores, query[low:high], 0, 0))
-
-        def whole(parts):
-            return jnp.concatenate([parts[0] + parts[1][:256], parts[1][256:]], axis=0)
-
-        grads = (whole(d_value), jnp.concatenate(d_query, axis=0), whole(d_key))
-        for kind, grad in enumerate(grads):
-            lanes = head_lanes(kind + 1, head)
-            rounded = grad.astype(BF16).astype(F32)
-            dpre_s[at, lanes] = (rounded * slope_s[at, lanes]).astype(BF16)
-        return 0
-
-    lax.fori_loop(0, 8, attend_back, 0, unroll=UNROLL)
-
-    def first_weight(part, _):
-        lanes = pl.ds(pl.multiple_of(part * 512, 512), 512)
-        wide = pl.ds(pl.multiple_of(part * 512 + 512, 512), 512)
-        g_ref[:, wide] = dot(norm_s[...], dpre_s[:, lanes], 0, 0).astype(BF16)
-        return 0
-
-    lax.fori_loop(0, 4, first_weight, 0)
-    stores[1].start()
-
-    def finish(s, _):
-        at = pl.ds(pl.multiple_of(s * SPAN, SPAN), SPAN)
-        d_normed = dot(dpre_s[at, 0:512], w_ref[:, 512:1024], 1, 1)
-        for part in range(1, 4):
-            lanes = slice(part * 512, part * 512 + 512)
-            wide = slice(part * 512 + 512, part * 512 + 1024)
-            d_normed = d_normed + dot(dpre_s[at, lanes], w_ref[:, wide], 1, 1)
-        normed, scale = moments(emb_s[at, :].astype(F32))
-        back = norm_back(d_normed.astype(BF16).astype(F32), normed, scale)
-        d_emb = (demb_s[at, :].astype(F32) + back).astype(BF16)
-        demb_s[at, :] = d_emb
-        d_rows = dot(d_emb, proj, 1, 1)
-        table = cols_ref[at, 1:2]
-        rank = cols_ref[at, 3:4]
-        lane = lax.broadcasted_iota(I32, (SPAN, half), 1)
-        kind = jnp.where(lane < 64, 0.0, 1.0)
-        for k in range(2):
-            match = rank == float(k)
-            low = k * 128
-            place_s[at, low : low + 128] = jnp.where(
-                (table == kind) & match, d_rows[:, 0:128], 0.0
-            ).astype(BF16)
-            place_s[at, 256 + low : 384 + low] = jnp.where(
-                (table == 2.0) & match, d_rows[:, 128:256], 0.0
-            ).astype(BF16)
-            low = 512 + k * 256
-            place_s[at, low : low + 256] = jnp.where(
-                (table == 3.0) & match, d_rows[:, 256:512], 0.0
-            ).astype(BF16)
-        return 0
-
-    lax.fori_loop(0, 2, finish, 0)
-    g_ref[:, 0:512] = dot(rows_s[...], demb_s[...], 0, 0).astype(BF16)
-    stores[0].start()
-    owner = cols_ref[:, 0:1].astype(I32)
-    hot = (owner == lax.broadcasted_iota(I32, (TOKENS, DEVICES), 1)).astype(BF16)
-    first_ref[...] = dot(hot, place_s[:, 0:512], 0, 0).astype(BF16)
-    second_ref[...] = dot(hot, place_s[:, 512:1024], 0, 0).astype(BF16)
-    for copy in stores:
-        copy.wait()
-
-
-def layer(got, cols, weights, cotangent):
-    def vmem(width, kind=BF16):
-        return pltpu.VMEM((TOKENS, width), kind)
-
-    return pl.pallas_call(
-        layer_kernel,
-        out_shape=(
-            jax.ShapeDtypeStruct((TOKENS, WIDTH), BF16),
-            jax.ShapeDtypeStruct((DEVICES, 512), BF16),
-            jax.ShapeDtypeStruct((DEVICES, 512), BF16),
-            jax.ShapeDtypeStruct((512, 3072), BF16),
-        ),
-        in_specs=[VM, VM, ANY, ANY],
-        out_specs=(ANY, VM, VM, ANY),
-        scratch_shapes=[
-            vmem(512), vmem(512), vmem(512), vmem(2048, F32), vmem(2048), vmem(512, F32),
-            vmem(512), vmem(512), vmem(2048), vmem(512), vmem(1024),
-            pltpu.VMEM((512, 3072), BF16), vmem(512), vmem(512), pltpu.VMEM((512, 3072), BF16),
-            pltpu.SemaphoreType.DMA((4,)), pltpu.SemaphoreType.DMA((4,)),
-        ],
-        compiler_params=pltpu.CompilerParams(vmem_limit_bytes=VMEM_LIMIT),
-        name="layer",
-    )(got, cols, weights, cotangent)
 
 
 def scatter_kernel(
@@ -746,51 +530,253 @@
     return total
 
 
-def deliver_kernel(
-    first_ref, second_ref, g_ref, rows_ref, total_ref,
+def core_kernel(
+    got_ref, cols_ref, w_hbm, cot_hbm, out_hbm, row_ref, total_ref,
+    rows_s, emb_s, norm_s, slope_s, act_s, att_s, gated_s, datt_s, dpre_s, demb_s, place_s,
+    w_ref, cot_ref, out_ref, in_sem, out_sem, first_ref, second_ref, g_ref,
     across, pair, one, two, line, three, four, parts, column, mine, whole, *scratch,
 ):
     dp, xy, core, z = place()
     (x, right, left, to_right, to_left), (y, up, down, to_up, to_down) = near()
     far_x, far_y = lax.rem(x + 2, NX), lax.rem(y + 2, NY)
     link = Sender(*scratch[-2:])
-    swap = Swap(link, first_ref, second_ref, rows_ref, *scratch[:-2])
-    swap.ready_high()
-    swap.ready_low()
-    greet(swap.along_z + swap.along_dp)
+    swap = Swap(link, first_ref, second_ref, row_ref, *scratch[:-2])
     partner = peers()[2][0]
     start = link.start
-
-    def meet(px, py, part):
-        there = (px, py, 1 - core, part)
-        return start(g_ref.at[there], across.at[px, py, part], partner)
-
-    def join(px, py, part):
+    everyone = swap.along_z + swap.along_dp
+    knock(everyone)
+    half = 128
+    pieces = (slice(0, 512), slice(512, 2560), slice(2560, 3072))
+    loads = [
+        pltpu.make_async_copy(w_hbm.at[:, part], w_ref.at[:, part], in_sem.at[i])
+        for i, part in enumerate(pieces)
+    ]
+    loads.append(pltpu.make_async_copy(cot_hbm, cot_ref, in_sem.at[3]))
+    for copy in loads:
+        copy.start()
+    store = pltpu.make_async_copy(out_ref, out_hbm, out_sem)
+
+    def term(value):
+        return value.reshape(NX, NY, 2, 2, 8, 512).astype(BF16)
+
+    loads[0].wait()
+    proj = w_ref[:, 0:512]
+
+    def begin(s, _):
+        at = pl.ds(pl.multiple_of(s * SPAN, SPAN), SPAN)
+        owner = cols_ref[at, 0:1].astype(I32)
+        table = cols_ref[at, 1:2]
+        rank = cols_ref[at, 3:4]
+        hot = (owner == lax.broadcasted_iota(I32, (SPAN, DEVICES), 1)).astype(BF16)
+        lane = lax.broadcasted_iota(I32, (SPAN, half), 1)
+        kind = jnp.where(lane < 64, 0.0, 1.0)
+        got = dot(hot, got_ref[0])
+        first = rank == 0.0
+        ab = jnp.where((table == kind), jnp.where(first, got[:, 0:128], got[:, 128:256]), 0.0)
+        c = jnp.where(table == 2.0, jnp.where(first, got[:, 256:384], got[:, 384:512]), 0.0)
+        got = dot(hot, got_ref[1])
+        d = jnp.where(table == 3.0, jnp.where(first, got[:, 0:256], got[:, 256:512]), 0.0)
+        rows = jnp.concatenate([ab, c, d], axis=1).astype(BF16)
+        rows_s[at, :] = rows
+        emb = dot(rows, proj).astype(BF16)
+        emb_s[at, :] = emb
+        normed, _scale = moments(emb.astype(F32))
+        norm_s[at, :] = normed.astype(BF16)
+        return 0
+
+    lax.fori_loop(0, 2, begin, 0)
+
+    loads[1].wait()
+
+    def project(i, _):
+        s, part = i // 4, lax.rem(i, 4)
+        at = pl.ds(pl.multiple_of(s * SPAN, SPAN), SPAN)
+        lanes = pl.ds(pl.multiple_of(part * 512, 512), 512)
+        pre = dot(norm_s[at, :], w_ref[:, pl.ds(pl.multiple_of(part * 512 + 512, 512), 512)])
+        sig = sigmoid(pre)
+        act = pre * sig
+        slope_s[at, lanes] = sig + act * (1.0 - sig)
+        act_s[at, lanes] = act.astype(BF16)
+        return 0
+
+    lax.fori_loop(0, 8, project, 0)
+
+    blocks = ((0, 256), (256, 384))
+
+    def head_lanes(kind, head):
+        return pl.ds(pl.multiple_of(kind * 512 + head * HEAD, HEAD), HEAD)
+
+    def kept(low, high, length):
+        row = lax.broadcasted_iota(I32, (high - low, high), 0) + low
+        column = lax.broadcasted_iota(I32, (high - low, high), 1)
+        return (column <= row) & (column.astype(F32) < length)
+
+    def attend(i, _):
+        s, head = i // 4, lax.rem(i, 4)
+        at = pl.ds(pl.multiple_of(s * SPAN, SPAN), SPAN)
+        length = cols_ref[at, 2:3]
+        value = act_s[at, head_lanes(1, head)]
+        query = act_s[at, head_lanes(2, head)]
+        key = act_s[at, head_lanes(3, head)]
+        results = []
+        for low, high in blocks:
+            scores = dot(query[low:high], key[:high], 1, 1) * HEAD**-0.5
+            keep = kept(low, high, length[low:high])
+            attn = jnp.where(keep, scores * sigmoid(scores), 0.0).astype(BF16)
+            results.append(dot(attn, value[:high]))
+        att_s[at, head_lanes(0, head)] = jnp.concatenate(results, axis=0)
+        return 0
+
+    lax.fori_loop(0, 8, attend, 0, unroll=UNROLL)
+    loads[2].wait()
+    loads[3].wait()
+    out_w = w_ref[:, 2560:3072]
+
+    def middle(s, _):
+        at = pl.ds(pl.multiple_of(s * SPAN, SPAN), SPAN)
+        normed, scale = moments(att_s[at, :])
+        gate = act_s[at, 0:512].astype(F32)
+        gated = (normed * gate).astype(BF16)
+        gated_s[at, :] = gated
+        branch = dot(gated, out_w)
+        out_ref[at, :] = (emb_s[at, :].astype(F32) + branch).astype(BF16)
+        where = lax.broadcasted_iota(I32, (SPAN, 1), 0).astype(F32)
+        grad = jnp.where(where < cols_ref[at, 2:3], cot_ref[at, :], jnp.zeros((), BF16))
+        demb_s[at, :] = grad
+        d_gated = dot(grad, out_w, 1, 1).astype(BF16).astype(F32)
+        d_gate = (d_gated * normed).astype(BF16).astype(F32)
+        dpre_s[at, 0:512] = (d_gate * slope_s[at, 0:512]).astype(BF16)
+        datt_s[at, :] = norm_back(d_gated * gate, normed, scale).astype(BF16)
+        return 0
+
+    lax.fori_loop(0, 2, middle, 0)
+    store.start()
+    g_ref[:, :, :, :, :, 2560:3072] = term(dot(gated_s[...], demb_s[...], 0, 0))
+
+    def attend_back(i, _):
+        s, head = i // 4, lax.rem(i, 4)
+        at = pl.ds(pl.multiple_of(s * SPAN, SPAN), SPAN)
+        length = cols_ref[at, 2:3]
+        value = act_s[at, head_lanes(1, head)]
+        query = act_s[at, head_lanes(2, head)]
+        key = act_s[at, head_lanes(3, head)]
+        d_att = datt_s[at, head_lanes(0, head)]
+        d_query, d_key, d_value = [], [], []
+        for low, high in blocks:
+            scores = dot(query[low:high], key[:high], 1, 1) * HEAD**-0.5
+            sig = sigmoid(scores)
+            act = scores * sig
+            keep = kept(low, high, length[low:high])
+            attn = jnp.where(keep, act, 0.0).astype(BF16)
+            d_attn = dot(d_att[low:high], value[:high], 1, 1).astype(BF16).astype(F32)
+            slope = sig + act * (1.0 - sig)
+            d_scores = (jnp.where(keep, d_attn * slope, 0.0) * HEAD**-0.5).astype(BF16)
+            d_value.append(dot(attn, d_att[low:high], 0, 0))
+            d_query.append(dot(d_scores, key[:high]))
+            d_key.append(dot(d_scores, query[low:high], 0, 0))
+
+        def whole(parts):
+            return jnp.concatenate([parts[0] + parts[1][:256], parts[1][256:]], axis=0)
+
+        grads = (whole(d_value), jnp.concatenate(d_query, axis=0), whole(d_key))
+        for kind, grad in enumerate(grads):
+            lanes = head_lanes(kind + 1, head)
+            rounded = grad.astype(BF16).astype(F32)
+            dpre_s[at, lanes] = (rounded * slope_s[at, lanes]).astype(BF16)
+        return 0
+
+    lax.fori_loop(0, 8, attend_back, 0, unroll=UNROLL)
+
+    def first_weight(part, _):
+        lanes = pl.ds(pl.multiple_of(part * 512, 512), 512)
+        wide = pl.ds(pl.multiple_of(part * 512 + 512, 512), 512)
+        g_ref[:, :, :, :, :, wide] = term(dot(norm_s[...], dpre_s[:, lanes], 0, 0))
+        return 0
+
+    lax.fori_loop(0, 4, first_weight, 0)
+    late, early = pl.ds(0, 512), pl.ds(512, 2560)
+
+    def meet(px, py, part, lanes):
+        source = g_ref.at[px, py, 1 - core, part, :, lanes]
+        return start(source, across.at[px, py, part, :, lanes], partner)
+
+    def meet_all(lanes):
+        far = [meet(far_x, EVERY, 0, lanes), meet(EVERY, far_y, 1, lanes)]
+        rest = [meet(side, EVERY, 0, lanes) for side in (right, left, x)]
+        return far, rest + [meet(EVERY, side, 1, lanes) for side in (up, down, y)]
+
+    def join(px, py, part, lanes):
         for k in range(4):
             qx, qy = (px, k) if py is EVERY else (k, py)
-            pair[qx, qy, part] = add(g_ref[qx, qy, core, part], across[qx, qy, part]).astype(BF16)
-
-    far = [meet(far_x, EVERY, 0), meet(EVERY, far_y, 1)]
+            pair[qx, qy, part, :, lanes] = add(
+                g_ref[qx, qy, core, part, :, lanes], across[qx, qy, part, :, lanes]
+            ).astype(BF16)
+
+    def send_far(lanes):
+        join(far_x, EVERY, 0, lanes)
+        join(EVERY, far_y, 1, lanes)
+        return [
+            start(pair.at[far_x, LOW, 0, :, lanes], one.at[0, :, :, lanes], to_right),
+            start(pair.at[far_x, HIGH, 0, :, lanes], one.at[1, :, :, lanes], to_left),
+            start(pair.at[LOW, far_y, 1, :, lanes], one.at[2, :, :, lanes], to_up),
+            start(pair.at[HIGH, far_y, 1, :, lanes], one.at[3, :, :, lanes], to_down),
+        ]
+
+    admit(everyone)
+    far, rest = meet_all(early)
+
+
+    def close(s):
+        at = slice(s * SPAN, s * SPAN + SPAN)
+        d_normed = dot(dpre_s[at, 0:512], w_ref[:, 512:1024], 1, 1)
+        for part in range(1, 4):
+            lanes = slice(part * 512, part * 512 + 512)
+            wide = slice(part * 512 + 512, part * 512 + 1024)
+            d_normed = d_normed + dot(dpre_s[at, lanes], w_ref[:, wide], 1, 1)
+        normed, scale = moments(emb_s[at, :].astype(F32))
+        back = norm_back(d_normed.astype(BF16).astype(F32), normed, scale)
+        d_emb = (demb_s[at, :].astype(F32) + back).astype(BF16)
+        demb_s[at, :] = d_emb
+        d_rows = dot(d_emb, proj, 1, 1)
+        table = cols_ref[at, 1:2]
+        rank = cols_ref[at, 3:4]
+        lane = lax.broadcasted_iota(I32, (SPAN, half), 1)
+        kind = jnp.where(lane < 64, 0.0, 1.0)
+        for k in range(2):
+            match = rank == float(k)
+            low = k * 128
+            place_s[at, low : low + 128] = jnp.where(
+                (table == kind) & match, d_rows[:, 0:128], 0.0
+            ).astype(BF16)
+            place_s[at, 256 + low : 384 + low] = jnp.where(
+                (table == 2.0) & match, d_rows[:, 128:256], 0.0
+            ).astype(BF16)
+            low = 512 + k * 256
+            place_s[at, low : low + 256] = jnp.where(
+                (table == 3.0) & match, d_rows[:, 256:512], 0.0
+            ).astype(BF16)
+
+    close(0)
+    finish(far)
+    steps = send_far(early)
+    close(1)
+    g_ref[:, :, :, :, :, 0:512] = term(dot(rows_s[...], demb_s[...], 0, 0))
+    far, more = meet_all(late)
+    owner = cols_ref[:, 0:1].astype(I32)
+    hot = (owner == lax.broadcasted_iota(I32, (TOKENS, DEVICES), 1)).astype(BF16)
+    first_ref[...] = dot(hot, place_s[:, 0:512], 0, 0).astype(BF16)
+    swap.ready_high()
     high = swap.begin_high()
-    sides = [
-        meet(right, EVERY, 0), meet(left, EVERY, 0), meet(EVERY, up, 1), meet(EVERY, down, 1)
-    ]
-    centre = [meet(x, EVERY, 0), meet(EVERY, y, 1)]
     finish(far)
-    join(far_x, EVERY, 0)
-    join(EVERY, far_y, 1)
-    steps = [
-        start(pair.at[far_x, LOW, 0], one.at[0], to_right),
-        start(pair.at[far_x, HIGH, 0], one.at[1], to_left),
-        start(pair.at[LOW, far_y, 1], one.at[2], to_up),
-        start(pair.at[HIGH, far_y, 1], one.at[3], to_down),
-    ]
+    steps += send_far(late)
+    second_ref[...] = dot(hot, place_s[:, 512:1024], 0, 0).astype(BF16).reshape(32, NZ, 512)
+    swap.ready_low()
     low = swap.begin_low()
-    finish(sides)
-    join(right, EVERY, 0)
-    join(left, EVERY, 0)
-    join(EVERY, up, 1)
-    join(EVERY, down, 1)
+    finish(rest + more)
+    for side in (right, left):
+        join(side, EVERY, 0, EVERY)
+    for side in (up, down):
+        join(EVERY, side, 1, EVERY)
     finish(steps)
     for k in range(2):
         pair[right, k, 0] = add(pair[right, k, 0], one[0, k]).astype(BF16)
@@ -805,9 +791,8 @@
     ]
     finish(low)
     low = swap.turn_low()
-    finish(centre)
-    join(x, EVERY, 0)
-    join(EVERY, y, 1)
+    join(x, EVERY, 0, EVERY)
+    join(EVERY, y, 1, EVERY)
     finish(steps)
     for k in range(4):
         line[0, k] = add(pair[x, k, 0], two[0, k], two[1, k]).astype(BF16)
@@ -848,18 +833,30 @@
     for half in range(2):
         for q in range(NZ):
             total_ref[half * 8 : half * 8 + 8, q * 384 : q * 384 + 384] = whole[q, half]
-
-
-def deliver(first, second, terms):
+    store.wait()
+
+
+def core(got, cols, weights, cotangent):
+    def vmem(width, kind=BF16):
+        return pltpu.VMEM((TOKENS, width), kind)
+
     return pl.pallas_call(
-        deliver_kernel,
+        core_kernel,
         out_shape=(
+            jax.ShapeDtypeStruct((TOKENS, WIDTH), BF16),
             jax.ShapeDtypeStruct((2, 32, 8, 512), BF16),
             jax.ShapeDtypeStruct((16, 3072), BF16),
         ),
-        in_specs=[VM] * 3,
-        out_specs=(VM, VM),
+        in_specs=[VM, VM, ANY, ANY],
+        out_specs=(ANY, VM, VM),
         scratch_shapes=[
+            vmem(512), vmem(512), vmem(512), vmem(2048, F32), vmem(2048), vmem(512, F32),
+            vmem(512), vmem(512), vmem(2048), vmem(512), vmem(1024),
+            pltpu.VMEM((512, 3072), BF16), vmem(512), vmem(512),
+            pltpu.SemaphoreType.DMA((4,)), pltpu.SemaphoreType.DMA,
+            pltpu.VMEM((DEVICES, 512), BF16),
+            pltpu.VMEM((32, 8, 512), BF16),
+            pltpu.VMEM((4, 4, 2, 2, 8, 3072), BF16),
             pltpu.VMEM((4, 4, 2, 8, 3072), BF16),
             pltpu.VMEM((4, 4, 2, 8, 3072), BF16),
             pltpu.VMEM((4, 2, 8, 3072), BF16),
@@ -873,10 +870,10 @@
             pltpu.VMEM((8, 2, 8, 384), BF16),
         ]
         + SWAP_SHAPES
-        + sems(114),
+        + sems(126),
         compiler_params=comm_params(3),
-        name="deliver",
-    )(first, second, terms)
+        name="core",
+    )(got, cols, weights, cotangent)
 
 
 def shards(
@@ -892,14 +889,11 @@
         (proj_weight, in_weight, out_weight),
         (table_a.T, table_b.T, table_c, table_d),
     )
-    output, first, second, terms = layer(
+    output, arrived, totals = core(
         got.reshape(2, DEVICES, 512),
         cols,
         full.reshape(512, 3072),
         cotangent.reshape(TOKENS, WIDTH),
-    )
-    arrived, totals = deliver(
-        first, second.reshape(32, 8, 512), terms.reshape(NX, NY, 2, 2, 8, 3072)
     )
     grads = scatter(arrived.reshape(2, DEVICES, 512), wanted, totals)
     return (

time: 130 us -> 123 us (0.946)
  Pallas kernels: 129 us -> 120 us
  local copies, waits for them, and re-layouts: 0 us -> 2.06 us
    pallas_call x2 -> x1, Pallas kernels: 71 us -> 61.5 us  [core(): pl.pallas_call(core_kernel, out_shape=(jax.ShapeDtypeStruct((TOKENS, WIDT...]
    unnamed x0 -> x1, local copies, waits for them, and re-layouts: none -> 2.06 us
where the time goes in v3:
time: 123 us; the launch traced here: 122 us
  Pallas kernels  120 us (98%)
  local copies, waits for them, and re-layouts  2.06 us (2%)
    pallas_call x1, Pallas kernels, core(): pl.pallas_call(core_kernel, out_shape=(jax.ShapeDtypeStruct((TOKENS, WIDT...  61.5 us
    pallas_call x1, Pallas kernels, front(): pl.pallas_call(front_kernel, out_shape=(jax.ShapeDtypeStruct((2, 32, 8, 5...  51.3 us
    pallas_call x1, Pallas kernels, scatter(): pl.pallas_call(scatter_kernel, out_shape=(jax.ShapeDtypeStruct((64, ROWS[...  6.86 us

profile of v3, /device:TPU:8, one launch (start us, length us, event | category | flops | bytes accessed | tf_op | source)
XLA Modules:
  0.0 122.4 jit_solution(5199193825557715455)
XLA Ops:
  0.6 51.3 %front.1 = (bf16[2,32,8,512]{3,2,1,0:T(8,128)(2,1)}, bf16[4,4,2,2,8,3072]{5,4,3,2,1,0:T(8,128)(2,1)}, f32[8,256]{1,0:T(8,128)}, f32[768,128]{1,0:T(8,128)}) custom-call(s32[2,384]{1,0:T(2,128)} %items_ref.1, s32[2,384]{1,0:T(2,128)} %tables_ref.1, s32[2]{0:T(128)} %lengths_ref.1, s32[2]{0:T(128)} %targets_ref.1, bf16[16,512]{1,0:T(8,128)(2,1)} %proj_ref.1, ...), custom_call_target="tpu_custom_call" | custom-call | tf_op jit(solution)/shard_map/front/pallas_call | solution.py:399
  52.0 61.5 %core.1 = (bf16[768,512]{1,0:T(8,128)(2,1)}, bf16[2,32,8,512]{3,2,1,0:T(8,128)(2,1)}, bf16[16,3072]{1,0:T(8,128)(2,1)}) custom-call(bf16[2,256,512]{2,1,0:T(8,128)(2,1)} %bitcast.14, f32[768,128]{1,0:T(8,128)} %get-tuple-element.23.cols_ref, bf16[512,3072]{1,0:T(8,128)(2,1)} %bitcast.9, bf16[768,512]{1,0:T(8,128)(2,1)} %bitcast.12), custom_call_target="tpu_custom_call" | custom-call | tf_op jit(solution)/shard_map/core/pallas_call | solution.py:843
  113.5 6.9 %scatter.1 = (bf16[64,12288]{1,0:T(8,128)(2,1)}, bf16[64,12288]{1,0:T(8,128)(2,1)}, bf16[6144,128]{1,0:T(8,128)(2,1)}, bf16[2048,256]{1,0:T(8,128)(2,1)}, f32[16...) custom-call(bf16[2,256,512]{2,1,0:T(8,128)(2,1)} %bitcast.15, f32[8,256]{1,0:T(8,128)} %get-tuple-element.27.wanted_ref, ...), custom_call_target="tpu_custom_call" | custom-call | tf_op jit(solution)/shard_map/scatter/pallas_call | solution.py:501
  120.4 2.1 %copy.21 = bf16[2,384,512]{2,1,0:T(8,128)(2,1)} copy(bf16[2,384,512]{2,1,0:T(8,128)(2,1)} %bitcast.13) | data formatting | bytes 1572864
